TPU v7x, 32 devices: a whole 2x2x4 slice. The times are simulated.
32 devices in a mesh: seq: 16 (over z, x, core), tp: 2 (over y).
Axes of the slice: x: 2, y: 2, z: 4, core: 2. Of those that a mesh axis runs over, the one named last changes fastest.
Arguments:
- hidden_in: bfloat16 [2048, 4096], P('seq', 'tp'), may hold values from -64 to 64
- span_order: int32 [16], replicated, may hold values from 0 to 15, each once
- norm_gain: bfloat16 [4096], P('tp'), may hold values from 0.099609375 to 1.8984375
- w_query: bfloat16 [4096, 4096], P('seq', 'tp'), may hold values from -0.09375 to 0.09375
- bias_query: bfloat16 [4096], P('tp'), may hold values from -14 to 14
- key_value_weight: bfloat16 [4096, 2, 1024], P('seq', None, 'tp'), may hold values from -0.09375 to 0.09375
- bias_kv: bfloat16 [2, 1024], P(None, 'tp'), may hold values from -14 to 14
- w_out: bfloat16 [4096, 4096], P('tp', 'seq'), may hold values from -0.09375 to 0.09375
- post_gain: bfloat16 [4096], P('tp'), may hold values from 0.099609375 to 1.8984375
Outputs:
- attn_out: bfloat16 [2048, 4096], P('seq', 'tp')
- normed: bfloat16 [2048, 4096], P('seq', 'tp')
Inputs may be any that keep to these rules, and one draw needn't show every extreme that they name: Each span number appears once; row r of hidden_in belongs to span span_order[r // 128].
All inputs are finite; a program needn't handle non-finite values.
Results may differ from a plain program's by a relative error of at most 0.014.
Values may be sent and summed in bfloat16 or wider, within the bound.
A program may use at most 128 MiB of HBM per device.

v0:
```python
import math

import jax
import jax.numpy as jnp
from jax import lax
from jax.experimental import pallas as pl
from jax.experimental.pallas import tpu as pltpu
from jax.sharding import PartitionSpec as P

MODEL_WIDTH = 4096
HEAD_SIZE = 128
GROUP = 4


eps = 1e-06
rope_base = 1000000.0


def apply_rotary(field, token_positions):
    half = field.shape[-1] // 2
    inverse = jnp.exp(-math.log(rope_base) * jnp.arange(half, dtype=jnp.float32) / half)
    angles = token_positions.astype(jnp.float32)[:, None] * inverse[None, :]
    cosine = jnp.cos(angles)[:, None, :]
    sine = jnp.sin(angles)[:, None, :]
    first = field[..., :half]
    second = field[..., half:]
    return jnp.concatenate(
        [first * cosine - second * sine, second * cosine + first * sine], axis=-1
    )


def span_lookup(order, devices):
    table_ids = jnp.arange(order.shape[0], dtype=jnp.int32)
    return jnp.sum(jnp.where(devices[:, None] == table_ids[None, :], order[None, :], 0), axis=1)


def per_device_by_span(
    hidden_in,
    span_order,
    norm_gain,
    w_query,
    bias_query,
    key_value_weight,
    bias_kv,
    w_out,
    post_gain,
):
    tok_rows = hidden_in.shape[0]
    seq_index = lax.axis_index("seq")
    own_span = span_lookup(span_order, jnp.full((1,), seq_index, jnp.int32))[0]
    token_positions = own_span * tok_rows + jnp.arange(tok_rows, dtype=jnp.int32)
    local = hidden_in.astype(jnp.float32)
    raw_rows, gains = (
        lax.all_gather(hidden_in, "tp", axis=1, tiled=True),
        lax.all_gather(norm_gain[None, :], "tp", axis=1, tiled=True),
    )
    full_rows = raw_rows.astype(jnp.float32)
    meansq = jnp.mean(full_rows * full_rows, axis=1, keepdims=True)
    normed_in = (full_rows * lax.rsqrt(meansq + eps) * gains.astype(jnp.float32)).astype(
        jnp.bfloat16
    )
    columns = normed_in
    query_proj = jnp.dot(
        columns,
        lax.all_gather(w_query, "seq", axis=0, tiled=True),
        preferred_element_type=jnp.float32,
    )
    columns = normed_in
    pair_proj = jnp.einsum(
        "tr,rkc->tkc",
        columns,
        lax.all_gather(key_value_weight, "seq", axis=0, tiled=True),
        preferred_element_type=jnp.float32,
    )
    query_heads = w_query.shape[1] // HEAD_SIZE
    kv_heads = key_value_weight.shape[2] // HEAD_SIZE
    query_proj = query_proj + bias_query.astype(jnp.float32)[None, :]
    queries = apply_rotary(
        query_proj.reshape(tok_rows, query_heads, HEAD_SIZE), token_positions
    ).astype(jnp.bfloat16)
    pair_proj = pair_proj + bias_kv.astype(jnp.float32)[None, :, :]
    rotated_keys = apply_rotary(
        pair_proj[:, 0, :].reshape(tok_rows, kv_heads, HEAD_SIZE), token_positions
    )
    rotated_keys = rotated_keys.astype(jnp.bfloat16).reshape(tok_rows, kv_heads * HEAD_SIZE)
    value_rows = pair_proj[:, 1, :].astype(jnp.bfloat16)
    grouped = (
        queries.reshape(tok_rows, kv_heads, GROUP, HEAD_SIZE)
        .transpose(1, 2, 0, 3)
        .reshape(kv_heads, GROUP * tok_rows, HEAD_SIZE)
    )
    query_pos = jnp.tile(token_positions, GROUP)
    last_query = jnp.max(token_positions)
    scale = 1.0 / math.sqrt(HEAD_SIZE)
    start_state = (
        jnp.full((kv_heads, GROUP * tok_rows), -1e30, jnp.float32),
        jnp.zeros((kv_heads, GROUP * tok_rows), jnp.float32),
        jnp.zeros((kv_heads, GROUP * tok_rows, HEAD_SIZE), jnp.float32),
    )
    key_piece = lax.all_gather(rotated_keys, "seq", axis=0, tiled=True)
    value_piece = lax.all_gather(value_rows, "seq", axis=0, tiled=True)
    count = key_piece.shape[0]
    block = math.gcd(count, 1536)

    def visit(step, state):
        first = step * block
        key_block = lax.dynamic_slice_in_dim(key_piece, first, block, 0).reshape(
            block, kv_heads, HEAD_SIZE
        )
        value_block = lax.dynamic_slice_in_dim(value_piece, first, block, 0).reshape(
            block, kv_heads, HEAD_SIZE
        )
        row_ids = first + jnp.arange(block, dtype=jnp.int32)
        key_pos = span_lookup(span_order, row_ids // tok_rows) * tok_rows + row_ids % tok_rows

        def update(current):
            maxima, totals, sums = current
            scores = (
                jnp.einsum("kqd,nkd->kqn", grouped, key_block, preferred_element_type=jnp.float32)
                * scale
            )
            allowed = (key_pos[None, :] <= query_pos[:, None])[None, :, :]
            scores = jnp.where(allowed, scores, -1e30)
            fresh = jnp.maximum(maxima, jnp.max(scores, axis=2))
            weights = jnp.where(allowed, jnp.exp(scores - fresh[:, :, None]), 0.0)
            factor = jnp.exp(maxima - fresh)
            totals = totals * factor + jnp.sum(weights, axis=2)
            sums = sums * factor[:, :, None] + jnp.einsum(
                "kqn,nkd->kqd",
                weights.astype(jnp.bfloat16),
                value_block,
                preferred_element_type=jnp.float32,
            )
            return (fresh, totals, sums)

        return lax.cond(jnp.min(key_pos) <= last_query, update, lambda current: current, state)

    maxima, totals, sums = lax.fori_loop(0, count // block, visit, start_state)
    attended = (sums / totals[:, :, None]).astype(jnp.bfloat16)
    attended = (
        attended.reshape(kv_heads, GROUP, tok_rows, HEAD_SIZE)
        .transpose(2, 0, 1, 3)
        .reshape(tok_rows, query_heads * HEAD_SIZE)
    )
    partial_out = jnp.dot(
        attended,
        lax.all_gather(w_out, "seq", axis=1, tiled=True),
        preferred_element_type=jnp.float32,
    )
    mixed = lax.psum_scatter(
        partial_out.astype(jnp.bfloat16), "tp", scatter_dimension=1, tiled=True
    ).astype(jnp.float32)
    attn_out = mixed.astype(jnp.bfloat16)
    stream = local + mixed
    post_sq = lax.psum(jnp.sum(stream * stream, axis=1), "tp")
    normed = (
        stream
        * lax.rsqrt(post_sq / MODEL_WIDTH + eps)[:, None]
        * post_gain.astype(jnp.float32)[None, :]
    ).astype(jnp.bfloat16)
    return (attn_out, normed)


def rope_tables(span_order, tok_rows):
    half = HEAD_SIZE // 2
    rows = (span_order[:, None] * tok_rows + jnp.arange(tok_rows, dtype=jnp.int32)[None, :]).reshape(-1)
    inverse = jnp.exp(-math.log(rope_base) * jnp.arange(half, dtype=jnp.float32) / half)
    angles = rows.astype(jnp.float32)[:, None] * inverse[None, :]
    cosine, sine = jnp.cos(angles), jnp.sin(angles)
    return (
        rows,
        jnp.concatenate([cosine, cosine], axis=1),
        jnp.concatenate([-sine, sine], axis=1),
    )


def attention_kernel(q_ref, k_ref, v_ref, qpos_ref, kpos_ref, out_ref):
    scores = lax.dot_general(
        q_ref[...], k_ref[...], (((1,), (1,)), ((), ())), preferred_element_type=jnp.float32
    ) * (1.0 / math.sqrt(HEAD_SIZE))
    allowed = kpos_ref[...] <= qpos_ref[...]
    scores = jnp.where(allowed, scores, -jnp.inf)
    peak = jnp.max(scores, axis=1, keepdims=True)
    weights = jnp.exp(scores - peak)
    totals = jnp.sum(weights, axis=1, keepdims=True)
    summed = jnp.dot(
        weights.astype(jnp.bfloat16), v_ref[...], preferred_element_type=jnp.float32
    )
    out_ref[...] = (summed / totals).astype(jnp.bfloat16)


def attention(queries, keys, values, positions):
    count = queries.shape[0]
    block = math.gcd(count, 256)
    rows = pl.BlockSpec((block, HEAD_SIZE), lambda i: (i, 0))
    whole = pl.BlockSpec((count, HEAD_SIZE), lambda i: (0, 0))
    return pl.pallas_call(
        attention_kernel,
        grid=(count // block,),
        in_specs=[
            rows,
            whole,
            whole,
            pl.BlockSpec((block, 1), lambda i: (i, 0)),
            pl.BlockSpec((1, count), lambda i: (0, 0)),
        ],
        out_specs=rows,
        out_shape=jax.ShapeDtypeStruct((count, HEAD_SIZE), jnp.bfloat16),
        cost_estimate=pl.CostEstimate(
            flops=4 * count * count * HEAD_SIZE,
            bytes_accessed=8 * count * HEAD_SIZE,
            transcendentals=count * count,
        ),
        name="attention",
    )(queries, keys, values, positions[:, None], positions[None, :])


MESH = pl.DeviceIdType.MESH
CORES = 2
PLANE = 4


class Traffic:
    def __init__(self, send_sem, peer):
        self.send_sem, self.peer, self.started = send_sem, peer, []

    def send(self, source, landing, arrival, target):
        copy = pltpu.make_async_remote_copy(
            src_ref=source,
            dst_ref=landing,
            send_sem=self.send_sem.at[len(self.started)],
            recv_sem=arrival,
            device_id=target,
            device_id_type=MESH,
        )
        copy.start()
        self.started.append(copy)

    def arrive(self, landing, arrival):
        pltpu.make_async_remote_copy(
            src_ref=landing,
            dst_ref=landing,
            send_sem=self.send_sem.at[0],
            recv_sem=arrival,
            device_id=self.peer,
            device_id_type=MESH,
        ).wait_recv()

    def finish(self):
        for copy in self.started:
            copy.wait_send()


def place(n_seq):
    s, t = lax.axis_index("seq"), lax.axis_index("tp")
    return s, t, s // PLANE, s % PLANE // CORES, s % CORES


def at(z, x, c):
    return z * PLANE + x * CORES + c


def exchange_kernel(
    n_seq, chunk, q_in, kv_in, rows_out, q_out, kv_out, local_sem, send_sem, rows_sem, q_sem, kv_sem
):
    s, t, z, x, c = place(n_seq)
    depth = n_seq // PLANE
    offset = s % PLANE
    sibling, across = (at(z, x, 1 - c), t), (at(z, 1 - x, c), t)
    other = (s, 1 - t)
    go = Traffic(send_sem, sibling)
    stay = [
        pltpu.make_async_copy(chunk, rows_out.at[s, t], local_sem.at[0]),
        pltpu.make_async_copy(q_in.at[s], q_out.at[s], local_sem.at[1]),
        pltpu.make_async_copy(kv_in.at[z], kv_out.at[s], local_sem.at[2]),
    ]
    for copy in stay:
        copy.start()

    def pass_on(source, owner, part, targets):
        for target in targets:
            go.send(source, rows_out.at[owner, part], rows_sem.at[owner, part], target)

    def await_rows(owner, part):
        go.arrive(rows_out.at[owner, part], rows_sem.at[owner, part])

    far = [lax.rem(z + d, depth) for d in range(1, depth)]
    near = [lax.rem(z - d + depth, depth) for d in range(depth)]
    pass_on(chunk, s, t, [other, across])
    pass_on(chunk, s, t, [(at(zt, x, c), t) for zt in far])
    pass_on(chunk, s, t, [sibling])
    for zt in far:
        target = at(zt, x, c)
        go.send(kv_in.at[zt], kv_out.at[s], kv_sem.at[s], (target, t))
    mates = [lax.rem(offset + r, PLANE) for r in range(1, PLANE)]
    for mate in mates:
        go.send(kv_in.at[z], kv_out.at[s], kv_sem.at[s], (z * PLANE + mate, t))
    for d in range(1, n_seq):
        target = lax.rem(s + d, n_seq)
        go.send(q_in.at[target], q_out.at[s], q_sem.at[s], (target, t))
    for zs in near[1:]:
        owner = at(zs, x, c)
        await_rows(owner, t)
        pass_on(rows_out.at[owner, t], owner, t, [other, across, sibling])
    for zs in near:
        owner = at(zs, 1 - x, c)
        await_rows(owner, t)
        pass_on(rows_out.at[owner, t], owner, t, [other, sibling])
    for zs in near[1:]:
        owner = at(zs, x, c)
        go.arrive(kv_out.at[owner], kv_sem.at[owner])
        for mate in mates:
            go.send(kv_out.at[owner], kv_out.at[owner], kv_sem.at[owner], (z * PLANE + mate, t))
    for xs in (x, 1 - x):
        for zs in near:
            owner = at(zs, xs, c)
            await_rows(owner, 1 - t)
            pass_on(rows_out.at[owner, 1 - t], owner, 1 - t, [sibling])
    for part in (t, 1 - t):
        for xs in (x, 1 - x):
            for zs in near:
                await_rows(at(zs, xs, 1 - c), part)
    for d in range(1, n_seq):
        owner = lax.rem(s - d + n_seq, n_seq)
        go.arrive(q_out.at[owner], q_sem.at[owner])
    for mate in mates:
        for zs in near:
            owner = zs * PLANE + mate
            go.arrive(kv_out.at[owner], kv_sem.at[owner])
    for copy in stay:
        copy.wait()
    go.finish()


def exchange(chunk, q_pieces, kv_pieces, n_seq, n_tp):
    vmem = pl.BlockSpec(memory_space=pltpu.VMEM)
    hbm = pl.BlockSpec(memory_space=pl.ANY)
    dma = pltpu.SemaphoreType.DMA
    return pl.pallas_call(
        lambda *refs: exchange_kernel(n_seq, *refs),
        out_shape=(
            jax.ShapeDtypeStruct((n_seq, n_tp) + chunk.shape, chunk.dtype),
            jax.ShapeDtypeStruct(q_pieces.shape, q_pieces.dtype),
            jax.ShapeDtypeStruct((n_seq,) + kv_pieces.shape[1:], kv_pieces.dtype),
        ),
        in_specs=[vmem] * 3,
        out_specs=(hbm,) * 3,
        scratch_shapes=[
            dma((3,)),
            dma((6 * n_seq,)),
            dma((n_seq, n_tp)),
            dma((n_seq,)),
            dma((n_seq,)),
        ],
        compiler_params=pltpu.CompilerParams(has_side_effects=True),
        cost_estimate=pl.CostEstimate(flops=0, bytes_accessed=16 * n_seq * n_tp * chunk.size, transcendentals=0),
        name="exchange",
    )(chunk, q_pieces, kv_pieces)


def heads_kernel(n_seq, chunk, heads_out, local_sem, send_sem, heads_sem):
    s, t, z, x, c = place(n_seq)
    depth = n_seq // PLANE
    sibling, across = (at(z, x, 1 - c), t), (at(z, 1 - x, c), t)
    go = Traffic(send_sem, sibling)
    stay = pltpu.make_async_copy(chunk.at[z], heads_out.at[s], local_sem.at[0])
    stay.start()
    near = [lax.rem(z - d + depth, depth) for d in range(depth)]
    for d in range(1, depth):
        zt = lax.rem(z + d, depth)
        go.send(chunk.at[zt], heads_out.at[s], heads_sem.at[s], (at(zt, x, c), t))
    for target in (across, sibling):
        go.send(chunk.at[z], heads_out.at[s], heads_sem.at[s], target)
    for zs in near[1:]:
        owner = at(zs, x, c)
        go.arrive(heads_out.at[owner], heads_sem.at[owner])
        for target in (across, sibling):
            go.send(heads_out.at[owner], heads_out.at[owner], heads_sem.at[owner], target)
    for zs in near:
        owner = at(zs, 1 - x, c)
        go.arrive(heads_out.at[owner], heads_sem.at[owner])
        go.send(heads_out.at[owner], heads_out.at[owner], heads_sem.at[owner], sibling)
    for xs in (x, 1 - x):
        for zs in near:
            owner = at(zs, xs, 1 - c)
            go.arrive(heads_out.at[owner], heads_sem.at[owner])
    stay.wait()
    go.finish()


def gather_heads(chunk, n_seq):
    dma = pltpu.SemaphoreType.DMA
    return pl.pallas_call(
        lambda *refs: heads_kernel(n_seq, *refs),
        out_shape=jax.ShapeDtypeStruct((n_seq,) + chunk.shape[1:], chunk.dtype),
        in_specs=[pl.BlockSpec(memory_space=pltpu.VMEM)],
        out_specs=pl.BlockSpec(memory_space=pl.ANY),
        scratch_shapes=[dma((1,)), dma((2 * n_seq,)), dma((n_seq,))],
        compiler_params=pltpu.CompilerParams(has_side_effects=True),
        name="gather_heads",
    )(chunk)


def mix_kernel(depth, heads, *refs):
    weights, out, flat = refs[:depth], refs[depth], refs[depth + 1]
    z = lax.axis_index("seq") // PLANE
    for head in range(heads.shape[0]):
        flat[:, head * HEAD_SIZE : (head + 1) * HEAD_SIZE] = heads[head]
    for d in range(depth):
        out[lax.rem(z - d + depth, depth)] = jnp.dot(
            flat[...], weights[d][...], preferred_element_type=jnp.float32
        ).astype(jnp.bfloat16)


def mix(heads, weights):
    n_heads, rows, size = heads.shape
    columns = weights[0].shape[1]
    vmem = pl.BlockSpec(memory_space=pltpu.VMEM)
    return pl.pallas_call(
        lambda *refs: mix_kernel(len(weights), *refs),
        out_shape=jax.ShapeDtypeStruct((len(weights), rows, columns), jnp.bfloat16),
        in_specs=[vmem] * (1 + len(weights)),
        out_specs=vmem,
        scratch_shapes=[pltpu.VMEM((rows, n_heads * size), jnp.bfloat16)],
        name="mix",
    )(heads, *weights)


def return_kernel(n_seq, n_tp, blocks, terms, local_sem, send_sem, terms_sem):
    s, t = lax.axis_index("seq"), lax.axis_index("tp")
    z, offset = s // PLANE, s % PLANE
    half = n_seq // PLANE // n_tp
    go = Traffic(send_sem, (s, 1 - t))

    def block(mate, goal):
        return blocks.at[pl.ds(goal * half, half), mate]

    pairs = [(r, q) for r in range(PLANE) for q in range(n_tp) if r or q]
    for r, q in pairs:
        mate, goal = lax.rem(offset + r, PLANE), lax.rem(t + q, n_tp)
        go.send(
            block(mate, goal), terms.at[t, offset], terms_sem.at[t, offset], (z * PLANE + mate, goal)
        )
    stay = pltpu.make_async_copy(block(offset, t), terms.at[t, offset], local_sem.at[0])
    stay.start()
    for r, q in pairs:
        mate, part = lax.rem(offset + r, PLANE), lax.rem(t + q, n_tp)
        go.arrive(terms.at[part, mate], terms_sem.at[part, mate])
    stay.wait()
    go.finish()


def return_blocks(blocks, n_seq, n_tp):
    dma = pltpu.SemaphoreType.DMA
    depth, mates, rows, columns = blocks.shape
    return pl.pallas_call(
        lambda *refs: return_kernel(n_seq, n_tp, *refs),
        out_shape=jax.ShapeDtypeStruct((n_tp, mates, depth // n_tp, rows, columns), blocks.dtype),
        in_specs=[pl.BlockSpec(memory_space=pltpu.VMEM)],
        out_specs=pl.BlockSpec(memory_space=pl.ANY),
        scratch_shapes=[dma((1,)), dma((n_tp * mates,)), dma((n_tp, mates))],
        compiler_params=pltpu.CompilerParams(has_side_effects=True),
        name="return_blocks",
    )(blocks)


def project_kernel(rows, wq, wkv, bias, cosine, sine, q_ref, k_ref, v_ref):
    spans, n_tp, span, width = rows.shape
    first, pair = bias[:, :HEAD_SIZE], bias[:, HEAD_SIZE:]
    query, both = first, pair
    for part in range(n_tp):
        piece = rows[:, part].reshape(spans * span, width)
        query = query + jnp.dot(
            piece, wq[pl.ds(part * width, width), :], preferred_element_type=jnp.float32
        )
        both = both + jnp.dot(
            piece, wkv[pl.ds(part * width, width), :], preferred_element_type=jnp.float32
        )

    def rotated(field):
        return (
            field * cosine[...] + pltpu.roll(field, HEAD_SIZE // 2, 1) * sine[...]
        ).astype(jnp.bfloat16)

    q_ref[...] = rotated(query)
    k_ref[...] = rotated(both[:, :HEAD_SIZE])
    v_ref[...] = both[:, HEAD_SIZE:].astype(jnp.bfloat16)


def project(rows, wq, wkv, bias, cosine, sine):
    n_seq, n_tp, span, width = rows.shape
    spans = math.gcd(n_seq, 4)
    table = pl.BlockSpec((spans * span, HEAD_SIZE), lambda i: (i, 0))
    whole = lambda a: pl.BlockSpec(a.shape, lambda i: (0, 0))
    out = jax.ShapeDtypeStruct((n_seq * span, HEAD_SIZE), jnp.bfloat16)
    return pl.pallas_call(
        project_kernel,
        grid=(n_seq // spans,),
        in_specs=[
            pl.BlockSpec((spans, n_tp, span, width), lambda i: (i, 0, 0, 0)),
            whole(wq),
            whole(wkv),
            whole(bias),
            table,
            table,
        ],
        out_specs=(table,) * 3,
        out_shape=(out,) * 3,
        cost_estimate=pl.CostEstimate(flops=6 * n_seq * n_tp * span * width * HEAD_SIZE, bytes_accessed=4 * rows.size, transcendentals=0),
        name="project",
    )(rows, wq, wkv, bias, cosine, sine)


def per_device_by_head(
    hidden_in,
    span_order,
    norm_gain,
    w_query,
    bias_query,
    key_value_weight,
    bias_kv,
    w_out,
    post_gain,
):
    tok_rows, width = hidden_in.shape
    n_seq = span_order.shape[0]
    n_tp = MODEL_WIDTH // width
    me = lax.axis_index("seq")
    slab = w_query.shape[0]
    kv_heads = key_value_weight.shape[2] // HEAD_SIZE
    share = n_seq // kv_heads
    q_pieces = w_query.reshape(slab, n_seq, HEAD_SIZE).transpose(1, 0, 2)
    kv_pieces = (
        key_value_weight.reshape(slab, 2, kv_heads, HEAD_SIZE)
        .transpose(2, 0, 1, 3)
        .reshape(kv_heads, slab, 2 * HEAD_SIZE)
    )
    local = hidden_in.astype(jnp.float32)
    meansq = lax.psum(jnp.sum(local * local, axis=1, keepdims=True), "tp") / MODEL_WIDTH
    normed_in = (
        local * lax.rsqrt(meansq + eps) * norm_gain.astype(jnp.float32)[None, :]
    ).astype(jnp.bfloat16)
    rows, wq, wkv = exchange(normed_in, q_pieces, kv_pieces, n_seq, n_tp)
    rows, wq, wkv, w_out = lax.optimization_barrier((rows, wq, wkv, w_out))
    depth = n_seq // PLANE
    out_weights = [w_out] + [
        lax.ppermute(w_out, "seq", [(i, (i + d * PLANE) % n_seq) for i in range(n_seq)])
        for d in range(1, depth)
    ]
    bias_q = lax.dynamic_slice_in_dim(bias_query, me * HEAD_SIZE, HEAD_SIZE)
    bias_pair = lax.dynamic_slice_in_dim(bias_kv, me // share * HEAD_SIZE, HEAD_SIZE, 1)
    bias = jnp.concatenate([bias_q, bias_pair[0], bias_pair[1]]).astype(jnp.float32)
    positions, cosine, sine = rope_tables(span_order, tok_rows)
    queries, keys, values = project(
        rows,
        wq.reshape(n_seq * slab, HEAD_SIZE),
        wkv.reshape(n_seq * slab, 2 * HEAD_SIZE),
        bias[None, :],
        cosine,
        sine,
    )
    attended = attention(queries, keys, values, positions)
    heads = gather_heads(attended.reshape(depth, PLANE * tok_rows, HEAD_SIZE), n_seq)
    partial_out = mix(heads, out_weights)
    columns = w_out.shape[1]
    terms = return_blocks(partial_out.reshape(depth, PLANE, tok_rows, columns), n_seq, n_tp)
    mixed = jnp.sum(terms.astype(jnp.float32), axis=0).transpose(2, 1, 0, 3).reshape(tok_rows, width)
    attn_out = mixed.astype(jnp.bfloat16)
    stream = local + mixed
    post_sq = lax.psum(jnp.sum(stream * stream, axis=1), "tp")
    normed = (
        stream
        * lax.rsqrt(post_sq / MODEL_WIDTH + eps)[:, None]
        * post_gain.astype(jnp.float32)[None, :]
    ).astype(jnp.bfloat16)
    return (attn_out, normed)


def per_device(*args):
    hidden_in, span_order, w_query, kv_weight = args[0], args[1], args[3], args[5]
    n_seq = span_order.shape[0]
    n_tp = MODEL_WIDTH // hidden_in.shape[1]
    heads = w_query.shape[1] // HEAD_SIZE
    kv_heads = kv_weight.shape[2] // HEAD_SIZE
    if n_tp == 2 and heads == n_seq and n_seq == kv_heads * GROUP and GROUP == PLANE and n_seq % (PLANE * n_tp) == 0:
        return per_device_by_head(*args)
    return per_device_by_span(*args)


def solution(mesh):
    placed = (
        P("seq", "tp"),
        P(),
        P("tp"),
        P("seq", "tp"),
        P("tp"),
        P("seq", None, "tp"),
        P(None, "tp"),
        P("tp", "seq"),
        P("tp"),
    )
    return jax.shard_map(
        per_device,
        mesh=mesh,
        in_specs=placed,
        out_specs=(P("seq", "tp"), P("seq", "tp")),
        check_vma=False,
    )
```

profile of v0, /device:TPU:8, one launch (start us, length us, event | category | flops | bytes accessed | tf_op | source)
XLA Modules:
  0.0 299.0 jit_solution(6170435474664284250)
XLA Ops:
  0.6 0.0 copy-start
  0.6 1.5 copy.16
  2.2 0.0 copy-start.5
  2.2 0.0 copy-start.1
  2.2 1.3 copy.17
  3.6 0.0 copy-done
  3.6 0.4 bitcast_bitcast_fusion
  3.9 1.1 reshape.134.refs_2_
  5.0 0.0 copy-done.5
  5.0 0.0 copy-start.2
  5.1 0.0 copy-start.7
  5.1 0.0 copy-done.1
  5.1 0.2 fusion
  5.3 5.1 %psum.14 = f32[128,1]{0,1:T(1,128)S(1)} all-reduce(f32[128,1]{0,1:T(1,128)S(1)} %bitcast.30), channel_id=1, replica_groups=mesh['seq'=16,'tp'=2] {'tp'}, use_global_device_ids=true, to_apply=%region_1.0 | all-reduce | flops 128 | bytes 1024 | tf_op jit(solution)/shard_map/psum | solution.py:539
  10.3 1.0 fusion.2.refs_0_
  11.3 133.6 %exchange.1 = (bf16[16,2,128,2048]{3,2,1,0:T(8,128)(2,1)}, bf16[16,256,128]{2,1,0:T(8,128)(2,1)}, bf16[16,256,256]{2,1,0:T(8,128)(2,1)}) custom-call(bf16[128,2048]{1,0:T(8,128)(2,1)} %fusion.2.refs_0_, bf16[16,256,128]{2,1,0:T(8,128)(2,1)} %bitcast.24, bf16[4,256,256]{2,1,0:T(8,128)(2,1)} %reshape.134.refs_2_), custom_call_target="tpu_custom_call" | custom-call | bytes 134217728 | tf_op jit(solution)/shard_map/exchange/pallas_call | solution.py:339
  144.9 0.0 copy-done.2
  144.9 0.1 collective-permute-start
  145.0 12.6 %collective-permute-start.1 = (bf16[2048,256]{1,0:T(8,128)(2,1)S(1)}, bf16[2048,256]{1,0:T(8,128)(2,1)}, u32[]{:S(2)}, u32[]{:S(2)}) collective-permute-start(bf16[2048,256]{1,0:T(8,128)(2,1)S(1)} %copy-done.2), channel_id=1, source_target_pairs={{0,16},{2,18},{4,20},{6,22},{8,24},{10,26},{12,28},{14,30},{16,0},... | collective-permute-start | bytes 3145736 | tf_op jit(solution)/shard_map/ppermute | solution.py:547
  157.6 1.9 collective-permute-start.2
  159.6 0.7 constant_dynamic-slice_fusion
  160.3 0.0 copy-done.7
  160.3 0.1 iota_add_fusion
  160.3 0.0 copy-start.4
  160.3 1.4 copy.19.qpos_ref
  161.7 0.8 dynamic-slice_bitcast_fusion
  162.5 3.7 %fusion.3 = (f32[2048,64]{1,0:T(8,128)S(1)}, f32[2048,64]{1,0:T(8,128)S(1)}, f32[2048,64]{1,0:T(8,128)S(1)}) fusion(f32[64]{0:T(128)S(1)} %multiply_exponential_fusion, f32[2048]{0:T(1024)S(1)} %get-tuple-element.28), kind=kLoop, calls=%fused_computation.14 | loop fusion | flops 262144 | bytes 1581312 | tf_op jit(solution)/shard_map/neg | solution.py:173
  166.2 0.0 copy-done.4
  166.2 0.5 maximum_convert_fusion.bias
  166.7 2.0 pad_maximum_fusion
  168.7 13.8 %project.1 = (bf16[2048,128]{1,0:T(8,128)(2,1)}, bf16[2048,128]{1,0:T(8,128)(2,1)}, bf16[2048,128]{1,0:T(8,128)(2,1)}) custom-call(bf16[16,2,128,2048]{3,2,1,0:T(8,128)(2,1)} %get-tuple-element.15.rows, bf16[4096,128]{1,0:T(8,128)(2,1)} %bitcast.32, bf16[4096,256]{1,0:T(8,128)(2,1)} %bitcast.31, f32[1,384]{1,0:T(1,128)} %maximum_convert_fusion.bias, ...), custom_call_target="tpu_custom_call" | custom-call | flops 6442450944 | bytes 33554432 | tf_op jit(solution)/shard_map/project/pallas_call | solution.py:496
  182.5 11.5 %attention.1 = bf16[2048,128]{1,0:T(8,128)(2,1)} custom-call(bf16[2048,128]{1,0:T(8,128)(2,1)} %get-tuple-element.18.q_ref, bf16[2048,128]{1,0:T(8,128)(2,1)} %get-tuple-element.19.k_ref, bf16[2048,128]{1,0:T(8,128)(2,1)} %get-tuple-element.20.v_ref, s32[2048,1]{1,0:T(8,128)} %copy.19.qpos_ref, s32[1,2048]{1,0:T(1,128)} %bitcast.29), custom_call_target="tpu_custom_call" | custom-call | flops 2147483648 | bytes 2097152 | tf_op jit(solution)/shard_map/attention/pallas_call | solution.py:197
  194.0 0.0 copy-start.6
  194.0 73.5 %gather_heads.1.refs_0_ = bf16[16,512,128]{2,1,0:T(8,128)(2,1)} custom-call(bf16[4,512,128]{2,1,0:T(8,128)(2,1)} %bitcast.27), custom_call_target="tpu_custom_call" | custom-call | tf_op jit(solution)/shard_map/gather_heads/pallas_call | solution.py:393
  267.5 0.0 copy-done.6
  267.6 0.0 collective-permute-done.refs_2_
  267.6 0.0 copy-start.3
  267.6 0.0 collective-permute-done.1.refs_3_
  267.6 0.0 collective-permute-done.2.refs_4_
  267.6 1.0 copy-done.3
  268.6 6.2 %mix.1 = bf16[4,512,256]{2,1,0:T(8,128)(2,1)} custom-call(bf16[16,512,128]{2,1,0:T(8,128)(2,1)} %gather_heads.1.refs_0_, bf16[2048,256]{1,0:T(8,128)(2,1)} %refs_1_, bf16[2048,256]{1,0:T(8,128)(2,1)} %copy-done.3, bf16[2048,256]{1,0:T(8,128)(2,1)} %collective-permute-done.1.refs_3_, bf16[2048,256]{1,0:T(8,128)(2,1)} %collective-permute-done.2.refs_4_), custom_call_target="tpu_custom_call" | custom-call | tf_op jit(solution)/shard_map/mix/pallas_call | solution.py:419
  274.7 15.2 %return_blocks.1 = bf16[2,4,2,128,256]{4,3,2,1,0:T(8,128)(2,1)} custom-call(bf16[4,4,128,256]{3,2,1,0:T(8,128)(2,1)} %bitcast.23), custom_call_target="tpu_custom_call" | custom-call | tf_op jit(solution)/shard_map/return_blocks/pallas_call | solution.py:456
  289.9 1.5 convert_reduce_fusion
  291.4 0.7 copy.20
  292.1 0.5 reshape.139
  292.6 0.2 multiply_reduce_fusion
  292.9 4.9 %psum.15 = f32[128]{0:T(128)S(1)} all-reduce(f32[128]{0:T(128)S(1)} %multiply_reduce_fusion), channel_id=1, replica_groups=mesh['seq'=16,'tp'=2] {'tp'}, use_global_device_ids=true, to_apply=%region_4.5 | all-reduce | flops 128 | bytes 1024 | tf_op jit(solution)/shard_map/psum | solution.py:570
  297.8 1.2 multiply_convert_fusion
  (7 shorter events, 0.0 us)
Async XLA Ops:
  0.6 2.9 copy-start
  2.2 2.9 copy-start.5
  2.2 2.9 copy-start.1
  5.0 139.9 %copy-start.2 = (bf16[2048,256]{1,0:T(8,128)(2,1)S(1)}, bf16[2048,256]{1,0:T(8,128)(2,1)}, u32[]{:S(2)}) copy-start(bf16[2048,256]{1,0:T(8,128)(2,1)} %refs_1_) | copy-start | bytes 3145732
  5.1 155.2 %copy-start.7 = (s32[16]{0:T(128)S(1)}, s32[16]{0:T(128)}, u32[]{:S(2)}) copy-start(s32[16]{0:T(128)} %param.10) | copy-start | bytes 196
  144.9 122.7 %collective-permute-start = (bf16[2048,256]{1,0:T(8,128)(2,1)S(1)}, bf16[2048,256]{1,0:T(8,128)(2,1)S(1)}, u32[]{:S(2)}, u32[]{:S(2)}) collective-permute-start(bf16[2048,256]{1,0:T(8,128)(2,1)S(1)} %copy-done.2), channel_id=1, source_target_pairs={{0,8},{2,10},{4,12},{6,14},{8,16},{10,18},{12,20},{14,22},{16,24},... | collective-permute-start | bytes 3145736 | tf_op jit(solution)/shard_map/ppermute | solution.py:547
  145.0 122.6 %collective-permute-start.1 = (bf16[2048,256]{1,0:T(8,128)(2,1)S(1)}, bf16[2048,256]{1,0:T(8,128)(2,1)}, u32[]{:S(2)}, u32[]{:S(2)}) collective-permute-start(bf16[2048,256]{1,0:T(8,128)(2,1)S(1)} %copy-done.2), channel_id=1, source_target_pairs={{0,16},{2,18},{4,20},{6,22},{8,24},{10,26},{12,28},{14,30},{16,0},... | collective-permute-start | bytes 3145736 | tf_op jit(solution)/shard_map/ppermute | solution.py:547
  157.6 110.0 %collective-permute-start.2 = (bf16[2048,256]{1,0:T(8,128)(2,1)S(1)}, bf16[2048,256]{1,0:T(8,128)(2,1)}, u32[]{:S(2)}, u32[]{:S(2)}) collective-permute-start(bf16[2048,256]{1,0:T(8,128)(2,1)S(1)} %copy-done.2), channel_id=1, source_target_pairs={{0,24},{2,26},{4,28},{6,30},{8,0},{10,2},{12,4},{14,6},{16,8},{18,... | collective-permute-start | bytes 3145736 | tf_op jit(solution)/shard_map/ppermute | solution.py:547
  160.3 5.8 %copy-start.4 = (s32[16,128]{1,0:T(8,128)}, s32[16,128]{1,0:T(8,128)S(1)}, u32[]{:S(2)}) copy-start(s32[16,128]{1,0:T(8,128)S(1)} %get-tuple-element.27) | copy-start | bytes 24580
  194.0 73.5 %copy-start.6 = (bf16[2048]{0:T(1024)(128)(2,1)S(1)}, bf16[2048]{0:T(1024)(128)(2,1)}, u32[]{:S(2)}) copy-start(bf16[2048]{0:T(1024)(128)(2,1)} %param.17) | copy-start | bytes 12292
  267.6 1.0 copy-start.3
where the time goes:
time: 302 us; the launch traced here: 299 us
  Pallas kernels  254 us (84%)
  starting transfers between devices  14.7 us (5%)
  other arithmetic  10.4 us (3%)
  blocking collectives  9.98 us (3%)
  local copies, waits for them, and re-layouts  9.35 us (3%)
    pallas_call x1, Pallas kernels, exchange(): pl.pallas_call(lambda *refs: exchange_kernel(n_seq, *refs), out_shape=(ja...  134 us
    pallas_call x1, Pallas kernels, gather_heads(): pl.pallas_call(lambda *refs: heads_kernel(n_seq, *refs), out_shape=jax.Sh...  73.5 us
    pallas_call x1, Pallas kernels, return_blocks(): pl.pallas_call(lambda *refs: return_kernel(n_seq, n_tp, *refs), out_shape...  15.2 us
    ppermute x3, starting transfers between devices, per_device_by_head(): lax.ppermute(w_out, 'seq', [(i, (i + d * PLANE) % n_seq) for i in range(n...  14.7 us
    pallas_call x1, Pallas kernels, project(): pl.pallas_call(project_kernel, grid=(n_seq // spans,), in_specs=[pl.Block...  13.8 us
    pallas_call x1, Pallas kernels, attention(): pl.pallas_call(attention_kernel, grid=(count // block,), in_specs=[rows,...  11.5 us
    pallas_call x1, Pallas kernels, mix(): pl.pallas_call(lambda *refs: mix_kernel(len(weights), *refs), out_shape=j...  6.15 us
  transfers between devices with their start and end apart: 3, of which 0 were waited for; matrix products, arithmetic and copies ran while one was open for 3% of the time, Pallas kernels for 33%

commit v1 on v0

v1 whole, which is shorter than its diff:
```python
import math

import jax
import jax.numpy as jnp
from jax import lax
from jax.experimental import pallas as pl
from jax.experimental.pallas import tpu as pltpu
from jax.sharding import PartitionSpec as P

MODEL_WIDTH = 4096
HEAD_SIZE = 128
GROUP = 4


eps = 1e-06
rope_base = 1000000.0


def apply_rotary(field, token_positions):
    half = field.shape[-1] // 2
    inverse = jnp.exp(-math.log(rope_base) * jnp.arange(half, dtype=jnp.float32) / half)
    angles = token_positions.astype(jnp.float32)[:, None] * inverse[None, :]
    cosine = jnp.cos(angles)[:, None, :]
    sine = jnp.sin(angles)[:, None, :]
    first = field[..., :half]
    second = field[..., half:]
    return jnp.concatenate(
        [first * cosine - second * sine, second * cosine + first * sine], axis=-1
    )


def span_lookup(order, devices):
    table_ids = jnp.arange(order.shape[0], dtype=jnp.int32)
    return jnp.sum(jnp.where(devices[:, None] == table_ids[None, :], order[None, :], 0), axis=1)


def per_device_by_span(
    hidden_in,
    span_order,
    norm_gain,
    w_query,
    bias_query,
    key_value_weight,
    bias_kv,
    w_out,
    post_gain,
):
    tok_rows = hidden_in.shape[0]
    seq_index = lax.axis_index("seq")
    own_span = span_lookup(span_order, jnp.full((1,), seq_index, jnp.int32))[0]
    token_positions = own_span * tok_rows + jnp.arange(tok_rows, dtype=jnp.int32)
    local = hidden_in.astype(jnp.float32)
    raw_rows, gains = (
        lax.all_gather(hidden_in, "tp", axis=1, tiled=True),
        lax.all_gather(norm_gain[None, :], "tp", axis=1, tiled=True),
    )
    full_rows = raw_rows.astype(jnp.float32)
    meansq = jnp.mean(full_rows * full_rows, axis=1, keepdims=True)
    normed_in = (full_rows * lax.rsqrt(meansq + eps) * gains.astype(jnp.float32)).astype(
        jnp.bfloat16
    )
    columns = normed_in
    query_proj = jnp.dot(
        columns,
        lax.all_gather(w_query, "seq", axis=0, tiled=True),
        preferred_element_type=jnp.float32,
    )
    columns = normed_in
    pair_proj = jnp.einsum(
        "tr,rkc->tkc",
        columns,
        lax.all_gather(key_value_weight, "seq", axis=0, tiled=True),
        preferred_element_type=jnp.float32,
    )
    query_heads = w_query.shape[1] // HEAD_SIZE
    kv_heads = key_value_weight.shape[2] // HEAD_SIZE
    query_proj = query_proj + bias_query.astype(jnp.float32)[None, :]
    queries = apply_rotary(
        query_proj.reshape(tok_rows, query_heads, HEAD_SIZE), token_positions
    ).astype(jnp.bfloat16)
    pair_proj = pair_proj + bias_kv.astype(jnp.float32)[None, :, :]
    rotated_keys = apply_rotary(
        pair_proj[:, 0, :].reshape(tok_rows, kv_heads, HEAD_SIZE), token_positions
    )
    rotated_keys = rotated_keys.astype(jnp.bfloat16).reshape(tok_rows, kv_heads * HEAD_SIZE)
    value_rows = pair_proj[:, 1, :].astype(jnp.bfloat16)
    grouped = (
        queries.reshape(tok_rows, kv_heads, GROUP, HEAD_SIZE)
        .transpose(1, 2, 0, 3)
        .reshape(kv_heads, GROUP * tok_rows, HEAD_SIZE)
    )
    query_pos = jnp.tile(token_positions, GROUP)
    last_query = jnp.max(token_positions)
    scale = 1.0 / math.sqrt(HEAD_SIZE)
    start_state = (
        jnp.full((kv_heads, GROUP * tok_rows), -1e30, jnp.float32),
        jnp.zeros((kv_heads, GROUP * tok_rows), jnp.float32),
        jnp.zeros((kv_heads, GROUP * tok_rows, HEAD_SIZE), jnp.float32),
    )
    key_piece = lax.all_gather(rotated_keys, "seq", axis=0, tiled=True)
    value_piece = lax.all_gather(value_rows, "seq", axis=0, tiled=True)
    count = key_piece.shape[0]
    block = math.gcd(count, 1536)

    def visit(step, state):
        first = step * block
        key_block = lax.dynamic_slice_in_dim(key_piece, first, block, 0).reshape(
            block, kv_heads, HEAD_SIZE
        )
        value_block = lax.dynamic_slice_in_dim(value_piece, first, block, 0).reshape(
            block, kv_heads, HEAD_SIZE
        )
        row_ids = first + jnp.arange(block, dtype=jnp.int32)
        key_pos = span_lookup(span_order, row_ids // tok_rows) * tok_rows + row_ids % tok_rows

        def update(current):
            maxima, totals, sums = current
            scores = (
                jnp.einsum("kqd,nkd->kqn", grouped, key_block, preferred_element_type=jnp.float32)
                * scale
            )
            allowed = (key_pos[None, :] <= query_pos[:, None])[None, :, :]
            scores = jnp.where(allowed, scores, -1e30)
            fresh = jnp.maximum(maxima, jnp.max(scores, axis=2))
            weights = jnp.where(allowed, jnp.exp(scores - fresh[:, :, None]), 0.0)
            factor = jnp.exp(maxima - fresh)
            totals = totals * factor + jnp.sum(weights, axis=2)
            sums = sums * factor[:, :, None] + jnp.einsum(
                "kqn,nkd->kqd",
                weights.astype(jnp.bfloat16),
                value_block,
                preferred_element_type=jnp.float32,
            )
            return (fresh, totals, sums)

        return lax.cond(jnp.min(key_pos) <= last_query, update, lambda current: current, state)

    maxima, totals, sums = lax.fori_loop(0, count // block, visit, start_state)
    attended = (sums / totals[:, :, None]).astype(jnp.bfloat16)
    attended = (
        attended.reshape(kv_heads, GROUP, tok_rows, HEAD_SIZE)
        .transpose(2, 0, 1, 3)
        .reshape(tok_rows, query_heads * HEAD_SIZE)
    )
    partial_out = jnp.dot(
        attended,
        lax.all_gather(w_out, "seq", axis=1, tiled=True),
        preferred_element_type=jnp.float32,
    )
    mixed = lax.psum_scatter(
        partial_out.astype(jnp.bfloat16), "tp", scatter_dimension=1, tiled=True
    ).astype(jnp.float32)
    attn_out = mixed.astype(jnp.bfloat16)
    stream = local + mixed
    post_sq = lax.psum(jnp.sum(stream * stream, axis=1), "tp")
    normed = (
        stream
        * lax.rsqrt(post_sq / MODEL_WIDTH + eps)[:, None]
        * post_gain.astype(jnp.float32)[None, :]
    ).astype(jnp.bfloat16)
    return (attn_out, normed)


MESH = pl.DeviceIdType.MESH
CORES = 2
PLANE = 4
PIECES = 2
PAIR = 2 * HEAD_SIZE


def at(z, x, c):
    return z * PLANE + x * CORES + c


class Traffic:
    def __init__(self, send_sem, peer):
        self.send_sem, self.peer, self.started = send_sem, peer, []

    def send(self, source, landing, arrival, target, when=None):
        index = len(self.started)

        def copy():
            return pltpu.make_async_remote_copy(
                src_ref=source,
                dst_ref=landing,
                send_sem=self.send_sem.at[index],
                recv_sem=arrival,
                device_id=target,
                device_id_type=MESH,
            )

        guarded(when, lambda: copy().start())
        self.started.append((when, copy))

    def arrive(self, landing, arrival, when=None):
        def wait():
            pltpu.make_async_remote_copy(
                src_ref=landing,
                dst_ref=landing,
                send_sem=self.send_sem.at[0],
                recv_sem=arrival,
                device_id=self.peer,
                device_id_type=MESH,
            ).wait_recv()

        guarded(when, wait)

    def finish(self):
        for when, copy in self.started:
            guarded(when, lambda: copy().wait_send())


def guarded(when, action):
    if when is None:
        action()
    else:
        pl.when(when)(action)


def both(first, second):
    return second if first is None else jnp.logical_and(first, second)


def rotate(field, cosine, sine):
    return field * cosine + pltpu.roll(field, HEAD_SIZE // 2, 1) * sine


def column_kernel(
    depth,
    hidden, order, gain, wq, bias_q, wkv, bias_kv, w_out, post_gain,
    attn_out, normed,
    rows, full, gains, weights, outw, kvs, queries, att, acc, part, terms, others, squares,
    kv_pieces, cos_t, sin_t, key_pos, bias_b, bias_p,
    local_sem, send_sem, rows_sem, gain_sem, w_sem, out_sem, kv_sem, att_sem, term_sem, other_sem, square_sem,
):
    s, t = lax.axis_index("seq"), lax.axis_index("tp")
    z, x, c = s // PLANE, s % PLANE // CORES, s % CORES
    span, half_width = hidden.shape
    slab = wq.shape[0]
    column = x * CORES + c
    sibling, across, other = (at(z, x, 1 - c), t), (at(z, 1 - x, c), t), (s, 1 - t)
    above, below = (at(jnp.minimum(z + 1, depth - 1), x, c), t), (at(jnp.maximum(z - 1, 0), x, c), t)

    barrier = pltpu.get_barrier_semaphore()
    peers = [sibling, across, other] + [(at(lax.rem(z + d, depth), x, c), t) for d in range(1, depth)]
    for peer in peers:
        pl.semaphore_signal(barrier, inc=1, device_id=peer, device_id_type=MESH)
    pl.semaphore_wait(barrier, len(peers))

    go = Traffic(send_sem, sibling)
    edge = span // PIECES

    def bit(p):
        return pl.ds(p * edge, edge)

    for p in range(PIECES):
        for target, when in ((other, None), (above, z < depth - 1), (below, z > 0)):
            go.send(hidden.at[bit(p)], rows.at[z, t, bit(p)], rows_sem.at[z, t, p], target, when)
    go.send(gain, gains.at[t], gain_sem.at[0], other)
    own = [
        pltpu.make_async_copy(hidden, rows.at[z, t], local_sem.at[0]),
        pltpu.make_async_copy(gain, gains.at[t], local_sem.at[1]),
        pltpu.make_async_copy(bias_q.at[:, pl.ds(pl.multiple_of(z * 2 * PAIR, PAIR), 2 * PAIR)], bias_b, local_sem.at[2]),
        pltpu.make_async_copy(bias_kv.at[:, pl.ds(pl.multiple_of(z * HEAD_SIZE, HEAD_SIZE), HEAD_SIZE)], bias_p, local_sem.at[3]),
        pltpu.make_async_copy(w_out, outw.at[column], local_sem.at[4]),
    ]

    def q_piece(g, zt):
        return wq.at[:, pl.ds(pl.multiple_of(zt * 2 * PAIR + (g - 1) * PAIR, PAIR), PAIR)]

    for g in (1, 2):
        own.append(pltpu.make_async_copy(q_piece(g, z), weights.at[g, s], local_sem.at[4 + g]))
    for copy in own:
        copy.start()
    for zt in range(depth):
        for i in range(2):
            kv_pieces[zt, :, i * HEAD_SIZE : (i + 1) * HEAD_SIZE] = wkv[:, i, zt * HEAD_SIZE : (zt + 1) * HEAD_SIZE]
    weights[0, s] = kv_pieces[z]
    for g in (0, 1, 2):
        source = kv_pieces.at[z] if g == 0 else q_piece(g, z)
        for target in (across, sibling):
            go.send(source, weights.at[g, s], w_sem.at[g, s], target)
    for target in (across, sibling):
        go.send(w_out, outw.at[column], out_sem.at[column], target)

    def spread(g, distance):
        for sign in (1, -1):
            zt = z + sign * distance
            when = jnp.logical_and(zt >= 0, zt < depth)
            zt = jnp.clip(zt, 0, depth - 1)
            source = kv_pieces.at[zt] if g == 0 else q_piece(g, zt)
            go.send(source, weights.at[g, s], w_sem.at[g, s], (at(zt, x, c), t), when)

    def chain(distance, action):
        for sign in (1, -1):
            zs = z - sign * distance
            when = jnp.logical_and(zs >= 0, zs < depth)
            zs = jnp.clip(zs, 0, depth - 1)
            target, more = (above, z < depth - 1) if sign == 1 else (below, z > 0)
            action(zs, when, target, jnp.logical_and(when, more))

    def pass_rows(distance):
        for p in range(PIECES):

            def action(zs, when, target, more):
                block, sem = rows.at[zs, t, bit(p)], rows_sem.at[zs, t, p]
                go.arrive(block, sem, when)
                go.send(block, block, sem, target, more)
                go.send(block, block, sem, other, when)

            chain(distance, action)

    def take_weights(g, distance):
        def action(zs, when, target, more):
            owner = at(zs, x, c)
            block, sem = weights.at[g, owner], w_sem.at[g, owner]
            go.arrive(block, sem, when)
            go.send(block, block, sem, across, when)
            go.send(block, block, sem, sibling, when)

        chain(distance, action)

    def weights_across(g):
        for zs in range(depth):
            owner = at(zs, 1 - x, c)
            block, sem = weights.at[g, owner], w_sem.at[g, owner]
            go.arrive(block, sem)
            go.send(block, block, sem, sibling)

    def weights_beside(g):
        for zs in range(depth):
            for xs in range(CORES):
                owner = at(zs, xs, 1 - c)
                go.arrive(weights.at[g, owner], w_sem.at[g, owner])

    def normalize(zs):
        for p in range(PIECES):
            go.arrive(rows.at[zs, 1 - t, bit(p)], rows_sem.at[zs, 1 - t, p])

        def strip(i, carry):
            r = pl.ds(pl.multiple_of(i * 16, 16), 16)
            halves = [rows[zs, h, r, :].astype(jnp.float32) for h in range(2)]
            total = sum(jnp.sum(a * a, axis=1, keepdims=True) for a in halves)
            factor = lax.rsqrt(total / (2 * half_width) + eps)
            for h in range(2):
                full[zs, r, h * half_width : (h + 1) * half_width] = (
                    halves[h] * factor * gains[h].astype(jnp.float32)
                ).astype(jnp.bfloat16)
            return carry

        lax.fori_loop(0, span // 16, strip, 0)

    lane = lax.broadcasted_iota(jnp.int32, (span, HEAD_SIZE), 1)
    line = lax.broadcasted_iota(jnp.int32, (span, HEAD_SIZE), 0)
    half = HEAD_SIZE // 2
    pair_id = jnp.where(lane < half, lane, lane - half).astype(jnp.float32)
    inverse = jnp.exp(-math.log(rope_base) * pair_id / half)

    def table(zs, carry):
        angles = (order[zs * PLANE + column] * span + line).astype(jnp.float32) * inverse
        cos_t[zs] = jnp.cos(angles)
        sine = jnp.sin(angles)
        sin_t[zs] = jnp.where(lane < half, -sine, sine)
        return carry

    lax.fori_loop(0, depth, table, 0)
    for m in range(PLANE):
        for zs in range(depth):
            i = m * depth + zs
            key_pos[:, i * span : (i + 1) * span] = order[zs * PLANE + m] * span + lax.broadcasted_iota(
                jnp.int32, (1, span), 1
            )
    for copy in own:
        copy.wait()
    go.arrive(gains.at[1 - t], gain_sem.at[0])

    pass_rows(1)
    spread(0, 1)
    spread(1, 1)
    normalize(z)
    pass_rows(2)
    for g in (0, 1):
        for distance in range(2, depth):
            spread(g, distance)
    for distance in range(1, depth):
        spread(2, distance)
    outw_across, outw_side = (1 - x) * CORES + c, 1 - c
    normalize(z + 1 - 2 * lax.rem(z, 2))
    take_weights(0, 1)
    pass_rows(3)
    take_weights(1, 1)
    for distance in range(2, depth):
        take_weights(0, distance)
    normalize(lax.rem(z + 2, depth))
    normalize(depth - 1 - z)
    go.arrive(outw.at[outw_across], out_sem.at[outw_across])
    go.send(outw.at[outw_across], outw.at[outw_across], out_sem.at[outw_across], sibling)
    weights_across(0)
    weights_beside(0)

    tokens = depth * span

    def product(g):
        return jnp.dot(
            full[...].reshape(tokens, 2 * half_width),
            weights[g].reshape(2 * half_width, PAIR),
            preferred_element_type=jnp.float32,
        )

    cosine, sine = cos_t[...].reshape(tokens, HEAD_SIZE), sin_t[...].reshape(tokens, HEAD_SIZE)
    pair = product(0)
    keys = pair[:, :HEAD_SIZE] + bias_p[0:1, :].astype(jnp.float32)
    kvs[column, :, :HEAD_SIZE] = rotate(keys, cosine, sine).astype(jnp.bfloat16)
    kvs[column, :, HEAD_SIZE:] = (pair[:, HEAD_SIZE:] + bias_p[1:2, :].astype(jnp.float32)).astype(jnp.bfloat16)
    for distance in range(2, depth):
        take_weights(1, distance)
    for target in (across, sibling):
        go.send(kvs.at[column], kvs.at[column], kv_sem.at[column], target)

    scale = math.log2(math.e) / math.sqrt(HEAD_SIZE)

    def make_queries(g):
        field = product(g)
        for i in range(2):
            cut = slice(i * HEAD_SIZE, (i + 1) * HEAD_SIZE)
            wide = slice((g - 1) * PAIR + i * HEAD_SIZE, (g - 1) * PAIR + (i + 1) * HEAD_SIZE)
            head = field[:, cut] + bias_b[:, wide].astype(jnp.float32)
            turned = (rotate(head, cosine, sine) * scale).astype(jnp.bfloat16)
            queries[g - 1, :, i * span : (i + 1) * span, :] = turned.reshape(depth, span, HEAD_SIZE)

    weights_across(1)
    weights_beside(1)
    make_queries(1)
    kv_across = (1 - x) * CORES + c
    go.arrive(kvs.at[kv_across], kv_sem.at[kv_across])
    go.send(kvs.at[kv_across], kvs.at[kv_across], kv_sem.at[kv_across], sibling)
    for distance in range(1, depth):
        take_weights(2, distance)
    for xs in range(CORES):
        owner = xs * CORES + 1 - c
        go.arrive(kvs.at[owner], kv_sem.at[owner])

    att_sends = 2 * 2 * depth

    def att_copy(g, b, side):
        target = above if side == 0 else below
        block = att.at[g, z, pl.ds(pl.multiple_of(b * span, span), span)]
        return pltpu.make_async_remote_copy(
            src_ref=block,
            dst_ref=block,
            send_sem=send_sem.at[send_sem.shape[0] - att_sends + (g * depth + b) * 2 + side],
            recv_sem=att_sem.at[g, z, b],
            device_id=target,
            device_id_type=MESH,
        )

    sides = ((0, z < depth - 1), (1, z > 0))

    def attend(g):
        def block(b, carry):
            scores = lax.dot_general(
                queries[g, b],
                kvs[:, :, :HEAD_SIZE].reshape(PLANE * tokens, HEAD_SIZE),
                (((1,), (1,)), ((), ())),
                preferred_element_type=jnp.float32,
            )
            first = order[b * PLANE + column] * span
            query_pos = first + lax.rem(lax.broadcasted_iota(jnp.int32, (2 * span, 1), 0), span)
            scores = jnp.where(key_pos[...] <= query_pos, scores, -jnp.inf)
            peak = jnp.max(scores, axis=1, keepdims=True)
            shares = jnp.exp2(scores - peak)
            totals = jnp.sum(shares, axis=1, keepdims=True)
            summed = jnp.dot(
                shares.astype(jnp.bfloat16),
                kvs[:, :, HEAD_SIZE:].reshape(PLANE * tokens, HEAD_SIZE),
                preferred_element_type=jnp.float32,
            )
            result = (summed / totals).astype(jnp.bfloat16)
            place = pl.ds(pl.multiple_of(b * span, span), span)
            att[g, z, place, :HEAD_SIZE] = result[:span]
            att[g, z, place, HEAD_SIZE:] = result[span:]
            for side, when in sides:
                pl.when(when)(lambda: att_copy(g, b, side).start())
            return carry

        lax.fori_loop(0, depth, block, 0)

    def pass_heads(g, distance):
        for b in range(depth):

            def action(zs, when, target, more):
                block, sem = att.at[g, zs, pl.ds(b * span, span)], att_sem.at[g, zs, b]
                go.arrive(block, sem, when)
                go.send(block, block, sem, target, more)

            chain(distance, action)

    attend(0)
    weights_across(2)
    pass_heads(0, 1)
    weights_beside(2)
    make_queries(2)
    attend(1)
    pass_heads(0, 2)
    pass_heads(1, 1)
    pass_heads(0, 3)
    for m in (outw_side, CORES + outw_side):
        go.arrive(outw.at[m], out_sem.at[m])

    def contribution(g, place, m):
        total = None
        for zs in range(depth):
            term = jnp.dot(
                att[g, zs, place, :],
                outw[m, zs * 2 * PAIR + g * PAIR : zs * 2 * PAIR + (g + 1) * PAIR, :],
                preferred_element_type=jnp.float32,
            )
            total = term if total is None else total + term
        return total

    width = w_out.shape[1]
    for m in range(PLANE):
        acc[:, m * width : (m + 1) * width] = contribution(0, slice(None), m)
    pass_heads(1, 2)
    pass_heads(1, 3)
    for d in (1, 2, 3, 0):
        zt = lax.rem(z + d, depth)
        place = pl.ds(pl.multiple_of(zt * span, span), span)
        for m in range(PLANE):
            cut = slice(m * width, (m + 1) * width)
            value = (acc[place, cut] + contribution(1, place, m)).astype(jnp.bfloat16)
            if d:
                part[zt, :, cut] = value
            else:
                terms[z, :, cut] = value
        if d:
            go.send(part.at[zt], terms.at[z], term_sem.at[z], (at(zt, x, c), t))

    share = depth // 2

    def cross(zs):
        goal = zs // share
        go.send(terms.at[zs], others.at[lax.rem(zs, share)], other_sem.at[lax.rem(zs, share)], other, goal != t)

    cross(z)
    for d in range(1, depth):
        zs = lax.rem(z - d + depth, depth)
        go.arrive(terms.at[zs], term_sem.at[zs])
        cross(zs)
    sums = jnp.zeros((span, 1), jnp.float32)
    wide = PLANE * width
    for j in range(share):
        go.arrive(others.at[j], other_sem.at[j])
        cut = slice(j * wide, (j + 1) * wide)
        mixed = terms[t * share + j].astype(jnp.float32) + others[j].astype(jnp.float32)
        attn_out[:, cut] = mixed.astype(jnp.bfloat16)
        stream = rows[z, t, :, cut].astype(jnp.float32) + mixed
        acc[pl.ds(j * span, span), :] = stream
        sums = sums + jnp.sum(stream * stream, axis=1, keepdims=True)
    squares[t] = jnp.broadcast_to(sums, (span, HEAD_SIZE))
    go.send(squares.at[t], squares.at[t], square_sem.at[0], other)
    go.arrive(squares.at[1 - t], square_sem.at[0])
    total = squares[0] + squares[1]
    factor = lax.rsqrt(total / (2 * half_width) + eps)[:, :1]
    for j in range(share):
        cut = slice(j * wide, (j + 1) * wide)
        normed[:, cut] = (
            acc[pl.ds(j * span, span), :] * factor * post_gain[:, cut].astype(jnp.float32)
        ).astype(jnp.bfloat16)
    assert len(go.started) + att_sends <= send_sem.shape[0]
    go.finish()
    for g in range(2):
        for b in range(depth):
            for side, when in sides:
                pl.when(when)(lambda: att_copy(g, b, side).wait_send())


def per_device_by_column(
    hidden_in,
    span_order,
    norm_gain,
    w_query,
    bias_query,
    key_value_weight,
    bias_kv,
    w_out,
    post_gain,
):
    span, half_width = hidden_in.shape
    n_seq = span_order.shape[0]
    depth = n_seq // PLANE
    slab = w_query.shape[0]
    tokens = depth * span
    vmem, hbm, smem = (pl.BlockSpec(memory_space=m) for m in (pltpu.VMEM, pl.ANY, pltpu.SMEM))
    dma = pltpu.SemaphoreType.DMA
    out = jax.ShapeDtypeStruct((span, half_width), jnp.bfloat16)
    bf16 = lambda *shape: pltpu.VMEM(shape, jnp.bfloat16)
    f32 = lambda *shape: pltpu.VMEM(shape, jnp.float32)
    width = w_out.shape[1]
    return pl.pallas_call(
        lambda *refs: column_kernel(depth, *refs),
        out_shape=(out, out),
        in_specs=[hbm, smem, vmem, hbm, hbm, vmem, hbm, hbm, vmem],
        out_specs=(vmem, vmem),
        scratch_shapes=[
            bf16(depth, 2, span, half_width),
            bf16(depth, span, 2 * half_width),
            bf16(2, 1, half_width),
            bf16(3, n_seq, slab, PAIR),
            bf16(PLANE, w_out.shape[0], width),
            bf16(PLANE, tokens, PAIR),
            bf16(2, depth, 2 * span, HEAD_SIZE),
            bf16(2, depth, tokens, PAIR),
            f32(tokens, PLANE * width),
            bf16(depth, span, PLANE * width),
            bf16(depth, span, PLANE * width),
            bf16(depth // 2, span, PLANE * width),
            f32(2, span, HEAD_SIZE),
            bf16(depth, slab, PAIR),
            f32(depth, span, HEAD_SIZE),
            f32(depth, span, HEAD_SIZE),
            pltpu.VMEM((1, PLANE * tokens), jnp.int32),
            bf16(1, 2 * PAIR),
            bf16(2, HEAD_SIZE),
            dma((8,)),
            dma((224,)),
            dma((depth, 2, PIECES)),
            dma((1,)),
            dma((3, n_seq)),
            dma((PLANE,)),
            dma((PLANE,)),
            dma((2, depth, depth)),
            dma((depth,)),
            dma((depth // 2,)),
            dma((1,)),
        ],
        compiler_params=pltpu.CompilerParams(
            collective_id=0, has_side_effects=True, vmem_limit_bytes=60 * 1024 * 1024
        ),
        name="sublayer",
    )(
        hidden_in,
        span_order,
        norm_gain[None, :],
        w_query,
        bias_query[None, :],
        key_value_weight,
        bias_kv,
        w_out,
        post_gain[None, :],
    )


def per_device(*args):
    hidden_in, span_order, w_query, kv_weight = args[0], args[1], args[3], args[5]
    n_seq = span_order.shape[0]
    n_tp = MODEL_WIDTH // hidden_in.shape[1]
    heads = w_query.shape[1] // HEAD_SIZE
    kv_heads = kv_weight.shape[2] // HEAD_SIZE
    if n_tp == 2 and n_seq == 4 * PLANE and kv_heads == 4 and heads == kv_heads * GROUP:
        return per_device_by_column(*args)
    return per_device_by_span(*args)


def solution(mesh):
    placed = (
        P("seq", "tp"),
        P(),
        P("tp"),
        P("seq", "tp"),
        P("tp"),
        P("seq", None, "tp"),
        P(None, "tp"),
        P("tp", "seq"),
        P("tp"),
    )
    return jax.shard_map(
        per_device,
        mesh=mesh,
        in_specs=placed,
        out_specs=(P("seq", "tp"), P("seq", "tp")),
        check_vma=False,
    )
```

time: 302 us -> 170 us (0.56); the launches traced: 299 us -> 170 us
  Pallas kernels: 254 us -> 164 us
  starting transfers between devices: 14.7 us -> 0 us
  other arithmetic: 10.4 us -> 0 us
  blocking collectives: 9.98 us -> 0 us
  local copies, waits for them, and re-layouts: 9.35 us -> 5.34 us
    pallas_call x6 -> x1, Pallas kernels: 254 us -> 164 us  [per_device_by_column(): pl.pallas_call(lambda *refs: column_kernel(depth, *refs), out_shape=(out,...]
    ppermute x3 -> x0, starting transfers between devices: 14.7 us -> none  [per_device_by_head(): lax.ppermute(w_out, 'seq', [(i, (i + d * PLANE) % n_seq) for i in range(n...]
    psum x2 -> x0, blocking collectives: 9.98 us -> none  [the longest x1 5.06 us: per_device_by_head(): lax.psum(jnp.sum(local * local, axis=1, keepdims=True), 'tp') / MODEL_WIDTH]
    neg x1 -> x0, other arithmetic: 3.72 us -> none  [rope_tables(): -sine]
  transfers between devices with their start and end apart: 3 -> 0, of which waited for: 0 -> 0; matrix products, arithmetic and copies ran while one was open for 3% -> 0% of each run, Pallas kernels for 33% -> 0%
where the time goes in v1:
time: 170 us
  Pallas kernels  164 us (96%)
  local copies, waits for them, and re-layouts  5.34 us (3%)
    pallas_call x1, Pallas kernels, per_device_by_column(): pl.pallas_call(lambda *refs: column_kernel(depth, *refs), out_shape=(out,...  164 us

profile of v1, /device:TPU:8, one launch (start us, length us, event | category | flops | bytes accessed | tf_op | source)
XLA Modules:
  0.0 170.2 jit_solution(960757817604246921)
XLA Ops:
  0.6 0.0 copy-start.1
  0.6 1.3 broadcast_in_dim.9.refs_2_
  1.9 0.0 copy-done.1
  1.9 0.0 copy-start.2
  1.9 0.6 broadcast_in_dim.10.refs_4_
  2.5 0.1 copy-done.2
  2.6 0.6 broadcast_in_dim.11.refs_8_
  3.2 164.2 %sublayer.1 = (bf16[128,2048]{1,0:T(8,128)(2,1)}, bf16[128,2048]{1,0:T(8,128)(2,1)}) custom-call(bf16[128,2048]{1,0:T(8,128)(2,1)} %refs_0_.1, s32[16]{0:T(128)} %refs_1_.1, bf16[1,2048]{1,0:T(2,128)(2,1)} %broadcast_in_dim.9.refs_2_, bf16[256,2048]{1,0:T(8,128)(2,1)} %refs_3_.1, bf16[1,2048]{1,0:T(2,128)(2,1)} %broadcast_in_dim.10.refs_4_, ...), custom_call_target="tpu_custom_call" | custom-call | tf_op jit(solution)/shard_map/sublayer/pallas_call | solution.py:600
  167.5 0.0 copy-start
  167.5 1.9 %copy.13 = bf16[128,2048]{1,0:T(8,128)(2,1)} copy(bf16[128,2048]{1,0:T(8,128)(2,1)} %get-tuple-element.4) | data formatting | bytes 1048576
  169.4 0.0 copy-done
  169.4 0.8 copy.14
Async XLA Ops:
  0.6 1.3 copy-start.1
  1.9 0.7 copy-start.2
  167.5 2.0 %copy-start = (bf16[128,2048]{1,0:T(8,128)(2,1)S(1)}, bf16[128,2048]{1,0:T(8,128)(2,1)}, u32[]{:S(2)}) copy-start(bf16[128,2048]{1,0:T(8,128)(2,1)} %get-tuple-element.5) | copy-start | bytes 1572868

commit v2 on v1

--- a/solution.py
+++ b/solution.py
@@ -173,41 +173,44 @@
 
 
 class Traffic:
-    def __init__(self, send_sem, peer):
-        self.send_sem, self.peer, self.started = send_sem, peer, []
-
-    def send(self, source, landing, arrival, target, when=None):
-        index = len(self.started)
-
-        def copy():
-            return pltpu.make_async_remote_copy(
-                src_ref=source,
-                dst_ref=landing,
-                send_sem=self.send_sem.at[index],
-                recv_sem=arrival,
-                device_id=target,
-                device_id_type=MESH,
-            )
-
-        guarded(when, lambda: copy().start())
-        self.started.append((when, copy))
+    def __init__(self, depth, z, sem, proxy, peer):
+        self.z, self.sem, self.proxy, self.peer = z, sem, proxy, peer
+        self.rows = [0] * depth
+
+    def remote(self, source, landing, arrival, target, sem=None):
+        return pltpu.make_async_remote_copy(
+            src_ref=source,
+            dst_ref=landing,
+            send_sem=self.sem.at[0] if sem is None else sem,
+            recv_sem=arrival,
+            device_id=target,
+            device_id_type=MESH,
+        )
+
+    def count(self, ref, where=None, times=1):
+        size = math.prod(ref.shape) * times // self.proxy.shape[1]
+        for k in range(len(self.rows)):
+            if where is None or where(k):
+                self.rows[k] += size
+
+    def send(self, source, landing, arrival, target, where=None, also=None, sem=None):
+        when = None if where is None else where(self.z)
+        if also is not None:
+            when = also if when is None else jnp.logical_and(when, also)
+        guarded(when, lambda: self.remote(source, landing, arrival, target, sem).start())
+        if sem is None and also is None:
+            self.count(source, where)
 
     def arrive(self, landing, arrival, when=None):
-        def wait():
-            pltpu.make_async_remote_copy(
-                src_ref=landing,
-                dst_ref=landing,
-                send_sem=self.send_sem.at[0],
-                recv_sem=arrival,
-                device_id=self.peer,
-                device_id_type=MESH,
-            ).wait_recv()
-
-        guarded(when, wait)
+        guarded(when, lambda: self.remote(landing, landing, arrival, self.peer).wait_recv())
+
+    def left(self, source, sem, when=None):
+        guarded(when, lambda: self.remote(source, source, sem, self.peer, sem).wait_send())
 
     def finish(self):
-        for when, copy in self.started:
-            guarded(when, lambda: copy().wait_send())
+        for k, size in enumerate(self.rows):
+            block = self.proxy.at[pl.ds(0, size)]
+            self.left(block, self.sem.at[0], self.z == k)
 
 
 def guarded(when, action):
@@ -217,29 +220,26 @@
         pl.when(when)(action)
 
 
-def both(first, second):
-    return second if first is None else jnp.logical_and(first, second)
-
-
 def rotate(field, cosine, sine):
     return field * cosine + pltpu.roll(field, HEAD_SIZE // 2, 1) * sine
 
 
 def column_kernel(
     depth,
-    hidden, order, gain, wq, bias_q, wkv, bias_kv, w_out, post_gain,
+    hidden, order, vectors, wq, wkv, bias_kv, w_out,
     attn_out, normed,
     rows, full, gains, weights, outw, kvs, queries, att, acc, part, terms, others, squares,
-    kv_pieces, cos_t, sin_t, key_pos, bias_b, bias_p,
-    local_sem, send_sem, rows_sem, gain_sem, w_sem, out_sem, kv_sem, att_sem, term_sem, other_sem, square_sem,
+    kv_pieces, cos_t, sin_t, key_pos, bias_b, bias_p, post_gain, proxy,
+    local_sem, send_sem, small_sem, relay_sem, rows_sem, rows_side_sem,
+    w_sem, w_across_sem, w_side_sem, out_sem, kv_sem, att_sem, term_sem, other_sem,
 ):
     s, t = lax.axis_index("seq"), lax.axis_index("tp")
     z, x, c = s // PLANE, s % PLANE // CORES, s % CORES
+    last = depth - 1
     span, half_width = hidden.shape
-    slab = wq.shape[0]
     column = x * CORES + c
     sibling, across, other = (at(z, x, 1 - c), t), (at(z, 1 - x, c), t), (s, 1 - t)
-    above, below = (at(jnp.minimum(z + 1, depth - 1), x, c), t), (at(jnp.maximum(z - 1, 0), x, c), t)
+    above, below = (at(jnp.minimum(z + 1, last), x, c), t), (at(jnp.maximum(z - 1, 0), x, c), t)
 
     barrier = pltpu.get_barrier_semaphore()
     peers = [sibling, across, other] + [(at(lax.rem(z + d, depth), x, c), t) for d in range(1, depth)]
@@ -247,22 +247,30 @@
         pl.semaphore_signal(barrier, inc=1, device_id=peer, device_id_type=MESH)
     pl.semaphore_wait(barrier, len(peers))
 
-    go = Traffic(send_sem, sibling)
+    go = Traffic(depth, z, send_sem, proxy, sibling)
+    gain, bias_q = vectors.at[0], vectors.at[1]
     edge = span // PIECES
 
     def bit(p):
         return pl.ds(p * edge, edge)
 
+    go.send(gain, gains.at[t], small_sem.at[0], other, sem=small_sem.at[1])
     for p in range(PIECES):
-        for target, when in ((other, None), (above, z < depth - 1), (below, z > 0)):
-            go.send(hidden.at[bit(p)], rows.at[z, t, bit(p)], rows_sem.at[z, t, p], target, when)
-    go.send(gain, gains.at[t], gain_sem.at[0], other)
+        mine, landing = hidden.at[bit(p)], rows.at[z, t, bit(p)]
+        go.send(mine, landing, rows_side_sem.at[z], other)
+        go.send(mine, landing, rows_sem.at[z, p], above, lambda k: k < last)
+        go.send(mine, landing, rows_sem.at[z, p], below, lambda k: k > 0)
     own = [
         pltpu.make_async_copy(hidden, rows.at[z, t], local_sem.at[0]),
         pltpu.make_async_copy(gain, gains.at[t], local_sem.at[1]),
-        pltpu.make_async_copy(bias_q.at[:, pl.ds(pl.multiple_of(z * 2 * PAIR, PAIR), 2 * PAIR)], bias_b, local_sem.at[2]),
-        pltpu.make_async_copy(bias_kv.at[:, pl.ds(pl.multiple_of(z * HEAD_SIZE, HEAD_SIZE), HEAD_SIZE)], bias_p, local_sem.at[3]),
+        pltpu.make_async_copy(
+            bias_q.at[:, pl.ds(pl.multiple_of(z * 2 * PAIR, PAIR), 2 * PAIR)], bias_b, local_sem.at[2]
+        ),
+        pltpu.make_async_copy(
+            bias_kv.at[:, pl.ds(pl.multiple_of(z * HEAD_SIZE, HEAD_SIZE), HEAD_SIZE)], bias_p, local_sem.at[3]
+        ),
         pltpu.make_async_copy(w_out, outw.at[column], local_sem.at[4]),
+        pltpu.make_async_copy(vectors.at[2], post_gain, local_sem.at[7]),
     ]
 
     def q_piece(g, zt):
@@ -278,64 +286,67 @@
     weights[0, s] = kv_pieces[z]
     for g in (0, 1, 2):
         source = kv_pieces.at[z] if g == 0 else q_piece(g, z)
-        for target in (across, sibling):
-            go.send(source, weights.at[g, s], w_sem.at[g, s], target)
-    for target in (across, sibling):
-        go.send(w_out, outw.at[column], out_sem.at[column], target)
-
-    def spread(g, distance):
-        for sign in (1, -1):
-            zt = z + sign * distance
-            when = jnp.logical_and(zt >= 0, zt < depth)
-            zt = jnp.clip(zt, 0, depth - 1)
-            source = kv_pieces.at[zt] if g == 0 else q_piece(g, zt)
-            go.send(source, weights.at[g, s], w_sem.at[g, s], (at(zt, x, c), t), when)
+        go.send(source, weights.at[g, s], w_across_sem.at[g], across)
+        go.send(source, weights.at[g, s], w_side_sem.at[g], sibling)
+    go.send(w_out, outw.at[column], out_sem.at[0], across)
+    go.send(w_out, outw.at[column], out_sem.at[1], sibling)
+
+    def spread(stage, groups):
+        for g in groups:
+            for zt, where in ((stage, lambda k: k < stage), (last - stage, lambda k: k > last - stage)):
+                source = kv_pieces.at[zt] if g == 0 else q_piece(g, zt)
+                go.send(source, weights.at[g, s], w_sem.at[g, z], (at(zt, x, c), t), where)
+
+    def take_weights(g, stage, distances=None):
+        for distance in distances or range(1, stage + 1):
+            for sign, goal in ((-1, stage), (1, last - stage)):
+                zs = jnp.clip(z + sign * distance, 0, last)
+                block = weights.at[g, at(zs, x, c)]
+                go.arrive(block, w_sem.at[g, zs], z == goal)
+                go.send(block, block, w_across_sem.at[g], across, lambda k: k == goal)
+                go.send(block, block, w_side_sem.at[g], sibling, lambda k: k == goal)
 
     def chain(distance, action):
         for sign in (1, -1):
-            zs = z - sign * distance
-            when = jnp.logical_and(zs >= 0, zs < depth)
-            zs = jnp.clip(zs, 0, depth - 1)
-            target, more = (above, z < depth - 1) if sign == 1 else (below, z > 0)
-            action(zs, when, target, jnp.logical_and(when, more))
+            zs = jnp.clip(z - sign * distance, 0, last)
+            where = lambda k: (k >= distance) if sign == 1 else (k + distance <= last)
+            target = above if sign == 1 else below
+            more = (lambda k: distance <= k < last) if sign == 1 else (lambda k: 0 < k <= last - distance)
+            if distance < last:
+                now = jnp.logical_and(z >= distance, z < last) if sign == 1 else jnp.logical_and(z > 0, z <= last - distance)
+                action(zs, where, target, (more, now))
+            else:
+                action(zs, where, target, None)
+
+    def relay(block, arrival, target, more, sem=None):
+        if more is not None:
+            where, now = more
+            pl.when(now)(lambda: go.remote(block, block, arrival, target, sem).start())
+            if sem is None:
+                go.count(block, where)
 
     def pass_rows(distance):
         for p in range(PIECES):
 
-            def action(zs, when, target, more):
-                block, sem = rows.at[zs, t, bit(p)], rows_sem.at[zs, t, p]
-                go.arrive(block, sem, when)
-                go.send(block, block, sem, target, more)
-                go.send(block, block, sem, other, when)
+            def action(zs, where, target, more):
+                block = rows.at[zs, t, bit(p)]
+                go.arrive(block, rows_sem.at[zs, p], where(z))
+                relay(block, rows_sem.at[zs, p], target, more, relay_sem.at[0] if distance == last - 1 else None)
+                go.send(block, block, rows_side_sem.at[zs], other, where)
 
             chain(distance, action)
 
-    def take_weights(g, distance):
-        def action(zs, when, target, more):
-            owner = at(zs, x, c)
-            block, sem = weights.at[g, owner], w_sem.at[g, owner]
-            go.arrive(block, sem, when)
-            go.send(block, block, sem, across, when)
-            go.send(block, block, sem, sibling, when)
-
-        chain(distance, action)
-
     def weights_across(g):
+        go.arrive(weights.at[g, pl.ds(0, depth)], w_across_sem.at[g])
         for zs in range(depth):
-            owner = at(zs, 1 - x, c)
-            block, sem = weights.at[g, owner], w_sem.at[g, owner]
-            go.arrive(block, sem)
-            go.send(block, block, sem, sibling)
+            block = weights.at[g, at(zs, 1 - x, c)]
+            go.send(block, block, w_side_sem.at[g], sibling)
 
     def weights_beside(g):
-        for zs in range(depth):
-            for xs in range(CORES):
-                owner = at(zs, xs, 1 - c)
-                go.arrive(weights.at[g, owner], w_sem.at[g, owner])
+        go.arrive(weights.at[g, pl.ds(0, depth * CORES)], w_side_sem.at[g])
 
     def normalize(zs):
-        for p in range(PIECES):
-            go.arrive(rows.at[zs, 1 - t, bit(p)], rows_sem.at[zs, 1 - t, p])
+        go.arrive(rows.at[zs, 1 - t], rows_side_sem.at[zs])
 
         def strip(i, carry):
             r = pl.ds(pl.multiple_of(i * 16, 16), 16)
@@ -372,29 +383,27 @@
             )
     for copy in own:
         copy.wait()
-    go.arrive(gains.at[1 - t], gain_sem.at[0])
-
+    go.arrive(gains.at[1 - t], small_sem.at[0])
+
+    middle = jnp.logical_and(z > 0, z < last)
     pass_rows(1)
-    spread(0, 1)
-    spread(1, 1)
+    spread(1, (0, 1, 2))
+    spread(3, (0,))
     normalize(z)
     pass_rows(2)
-    for g in (0, 1):
-        for distance in range(2, depth):
-            spread(g, distance)
-    for distance in range(1, depth):
-        spread(2, distance)
-    outw_across, outw_side = (1 - x) * CORES + c, 1 - c
+    spread(2, (0, 1, 2))
+    for g in (0, 1, 2):
+        take_weights(g, 1)
     normalize(z + 1 - 2 * lax.rem(z, 2))
-    take_weights(0, 1)
+    take_weights(0, 3)
+    go.left(rows.at[z, t], relay_sem.at[0], middle)
     pass_rows(3)
-    take_weights(1, 1)
-    for distance in range(2, depth):
-        take_weights(0, distance)
+    spread(3, (1, 2))
+    for g in (0, 1, 2):
+        take_weights(g, 2)
     normalize(lax.rem(z + 2, depth))
-    normalize(depth - 1 - z)
-    go.arrive(outw.at[outw_across], out_sem.at[outw_across])
-    go.send(outw.at[outw_across], outw.at[outw_across], out_sem.at[outw_across], sibling)
+    take_weights(1, 3, (1, 2))
+    normalize(last - z)
     weights_across(0)
     weights_beside(0)
 
@@ -412,10 +421,10 @@
     keys = pair[:, :HEAD_SIZE] + bias_p[0:1, :].astype(jnp.float32)
     kvs[column, :, :HEAD_SIZE] = rotate(keys, cosine, sine).astype(jnp.bfloat16)
     kvs[column, :, HEAD_SIZE:] = (pair[:, HEAD_SIZE:] + bias_p[1:2, :].astype(jnp.float32)).astype(jnp.bfloat16)
-    for distance in range(2, depth):
-        take_weights(1, distance)
-    for target in (across, sibling):
-        go.send(kvs.at[column], kvs.at[column], kv_sem.at[column], target)
+    go.send(kvs.at[column], kvs.at[column], kv_sem.at[0], across)
+    go.send(kvs.at[column], kvs.at[column], kv_sem.at[1], sibling)
+    take_weights(1, 3, (3,))
+    take_weights(2, 3)
 
     scale = math.log2(math.e) / math.sqrt(HEAD_SIZE)
 
@@ -431,33 +440,20 @@
     weights_across(1)
     weights_beside(1)
     make_queries(1)
-    kv_across = (1 - x) * CORES + c
-    go.arrive(kvs.at[kv_across], kv_sem.at[kv_across])
-    go.send(kvs.at[kv_across], kvs.at[kv_across], kv_sem.at[kv_across], sibling)
-    for distance in range(1, depth):
-        take_weights(2, distance)
-    for xs in range(CORES):
-        owner = xs * CORES + 1 - c
-        go.arrive(kvs.at[owner], kv_sem.at[owner])
-
-    att_sends = 2 * 2 * depth
-
-    def att_copy(g, b, side):
-        target = above if side == 0 else below
-        block = att.at[g, z, pl.ds(pl.multiple_of(b * span, span), span)]
-        return pltpu.make_async_remote_copy(
-            src_ref=block,
-            dst_ref=block,
-            send_sem=send_sem.at[send_sem.shape[0] - att_sends + (g * depth + b) * 2 + side],
-            recv_sem=att_sem.at[g, z, b],
-            device_id=target,
-            device_id_type=MESH,
-        )
-
-    sides = ((0, z < depth - 1), (1, z > 0))
+    kv_across = kvs.at[(1 - x) * CORES + c]
+    go.arrive(kv_across, kv_sem.at[0])
+    go.send(kv_across, kv_across, kv_sem.at[1], sibling)
+    go.arrive(kvs.at[pl.ds(0, CORES)], kv_sem.at[1])
+
+    def att_piece(g, zs, b):
+        return att.at[g, zs, pl.ds(pl.multiple_of(b * span, span), span)]
+
+    def nth(i):
+        return jnp.where(i == 0, 0, jnp.where(i == 1, last, jnp.where(i == 2, 1 + c, 2 - c)))
 
     def attend(g):
-        def block(b, carry):
+        def turn(i, carry):
+            b = nth(i)
             scores = lax.dot_general(
                 queries[g, b],
                 kvs[:, :, :HEAD_SIZE].reshape(PLANE * tokens, HEAD_SIZE),
@@ -479,100 +475,112 @@
             place = pl.ds(pl.multiple_of(b * span, span), span)
             att[g, z, place, :HEAD_SIZE] = result[:span]
             att[g, z, place, HEAD_SIZE:] = result[span:]
-            for side, when in sides:
-                pl.when(when)(lambda: att_copy(g, b, side).start())
+            block = att_piece(g, z, b)
+            pl.when(z < last)(lambda: go.remote(block, block, att_sem.at[g, z, b], above).start())
+            pl.when(z > 0)(lambda: go.remote(block, block, att_sem.at[g, z, b], below).start())
             return carry
 
-        lax.fori_loop(0, depth, block, 0)
-
-    def pass_heads(g, distance):
-        for b in range(depth):
-
-            def action(zs, when, target, more):
-                block, sem = att.at[g, zs, pl.ds(b * span, span)], att_sem.at[g, zs, b]
-                go.arrive(block, sem, when)
-                go.send(block, block, sem, target, more)
-
-            chain(distance, action)
+        lax.fori_loop(0, depth, turn, 0)
+        go.count(att.at[g, 0], lambda k: k < last)
+        go.count(att.at[g, 0], lambda k: k > 0)
 
     attend(0)
     weights_across(2)
-    pass_heads(0, 1)
     weights_beside(2)
     make_queries(2)
     attend(1)
-    pass_heads(0, 2)
-    pass_heads(1, 1)
-    pass_heads(0, 3)
-    for m in (outw_side, CORES + outw_side):
-        go.arrive(outw.at[m], out_sem.at[m])
-
-    def contribution(g, place, m):
-        total = None
-        for zs in range(depth):
-            term = jnp.dot(
-                att[g, zs, place, :],
-                outw[m, zs * 2 * PAIR + g * PAIR : zs * 2 * PAIR + (g + 1) * PAIR, :],
-                preferred_element_type=jnp.float32,
-            )
-            total = term if total is None else total + term
-        return total
+    outw_across = outw.at[(1 - x) * CORES + c]
+    go.arrive(outw_across, out_sem.at[0])
+    go.send(outw_across, outw_across, out_sem.at[1], sibling)
+    go.arrive(outw.at[pl.ds(0, CORES)], out_sem.at[1])
+
+    def pass_heads(g, b, distance):
+        def action(zs, where, target, more):
+            block, sem = att_piece(g, zs, b), att_sem.at[g, zs, b]
+            go.arrive(block, sem, where(z))
+            relay(block, sem, target, more)
+
+        chain(distance, action)
+
+    halves = 2
+    each = PLANE // halves
+
+    def piece(ref, i, h):
+        return ref.at[i, pl.ds(h * each, each)]
+
+    def mix_block(b):
+        place = pl.ds(pl.multiple_of(b * span, span), span)
+        for h in range(halves):
+            for m in range(h * each, (h + 1) * each):
+                total = None
+                for zs in range(depth):
+                    for g in range(2):
+                        first = zs * 2 * PAIR + g * PAIR
+                        term = jnp.dot(
+                            att[g, zs, place, :], outw[m, first : first + PAIR, :], preferred_element_type=jnp.float32
+                        )
+                        total = term if total is None else total + term
+                value = total.astype(jnp.bfloat16)
+
+                @pl.when(b == z)
+                def _():
+                    terms[z, m] = value
+
+                @pl.when(b != z)
+                def _():
+                    part[b, m] = value
+
+            @pl.when(b != z)
+            def _():
+                go.remote(piece(part, b, h), piece(terms, z, h), term_sem.at[z, h], (at(b, x, c), t)).start()
+
+    share = depth // 2
+
+    def settle():
+        for zs in (1, 2, 0, 3):
+            for h in range(halves):
+                block = piece(terms, zs, h)
+                go.arrive(block, term_sem.at[zs, h], z != zs)
+                landing, sem = piece(others, zs % share, h), other_sem.at[zs % share, h]
+                go.send(block, landing, sem, other, also=t != zs // share)
+
+    for g in range(2):
+        for i in range(depth):
+            pass_heads(g, nth(i), 1)
+    for i in range(depth):
+        for g in range(2):
+            pass_heads(g, nth(i), 2)
+    for i in range(depth):
+        for g in range(2):
+            pass_heads(g, nth(i), 3)
+        mix_block(nth(i))
+    settle()
+    go.count(part.at[0], times=depth - 1)
+    go.count(others.at[0], times=share)
 
     width = w_out.shape[1]
-    for m in range(PLANE):
-        acc[:, m * width : (m + 1) * width] = contribution(0, slice(None), m)
-    pass_heads(1, 2)
-    pass_heads(1, 3)
-    for d in (1, 2, 3, 0):
-        zt = lax.rem(z + d, depth)
-        place = pl.ds(pl.multiple_of(zt * span, span), span)
-        for m in range(PLANE):
-            cut = slice(m * width, (m + 1) * width)
-            value = (acc[place, cut] + contribution(1, place, m)).astype(jnp.bfloat16)
-            if d:
-                part[zt, :, cut] = value
-            else:
-                terms[z, :, cut] = value
-        if d:
-            go.send(part.at[zt], terms.at[z], term_sem.at[z], (at(zt, x, c), t))
-
-    share = depth // 2
-
-    def cross(zs):
-        goal = zs // share
-        go.send(terms.at[zs], others.at[lax.rem(zs, share)], other_sem.at[lax.rem(zs, share)], other, goal != t)
-
-    cross(z)
-    for d in range(1, depth):
-        zs = lax.rem(z - d + depth, depth)
-        go.arrive(terms.at[zs], term_sem.at[zs])
-        cross(zs)
     sums = jnp.zeros((span, 1), jnp.float32)
-    wide = PLANE * width
-    for j in range(share):
-        go.arrive(others.at[j], other_sem.at[j])
-        cut = slice(j * wide, (j + 1) * wide)
-        mixed = terms[t * share + j].astype(jnp.float32) + others[j].astype(jnp.float32)
+    pieces = [(j, m) for j in range(share) for m in range(PLANE)]
+    for j, m in pieces:
+        if m % each == 0:
+            go.arrive(piece(others, j, m // each), other_sem.at[j, m // each])
+        cut = slice((j * PLANE + m) * width, (j * PLANE + m + 1) * width)
+        mixed = terms[t * share + j, m].astype(jnp.float32) + others[j, m].astype(jnp.float32)
         attn_out[:, cut] = mixed.astype(jnp.bfloat16)
         stream = rows[z, t, :, cut].astype(jnp.float32) + mixed
-        acc[pl.ds(j * span, span), :] = stream
+        acc[j, m] = stream
         sums = sums + jnp.sum(stream * stream, axis=1, keepdims=True)
-    squares[t] = jnp.broadcast_to(sums, (span, HEAD_SIZE))
-    go.send(squares.at[t], squares.at[t], square_sem.at[0], other)
-    go.arrive(squares.at[1 - t], square_sem.at[0])
-    total = squares[0] + squares[1]
+    squares[t] = jnp.broadcast_to(sums, (span, span)).T[:8]
+    go.send(squares.at[t], squares.at[t], small_sem.at[2], other, sem=small_sem.at[3])
+    go.arrive(squares.at[1 - t], small_sem.at[2])
+    total = jnp.broadcast_to((squares[0] + squares[1])[:1], (span, span)).T
     factor = lax.rsqrt(total / (2 * half_width) + eps)[:, :1]
-    for j in range(share):
-        cut = slice(j * wide, (j + 1) * wide)
-        normed[:, cut] = (
-            acc[pl.ds(j * span, span), :] * factor * post_gain[:, cut].astype(jnp.float32)
-        ).astype(jnp.bfloat16)
-    assert len(go.started) + att_sends <= send_sem.shape[0]
+    for j, m in pieces:
+        cut = slice((j * PLANE + m) * width, (j * PLANE + m + 1) * width)
+        normed[:, cut] = (acc[j, m] * factor * post_gain[:, cut].astype(jnp.float32)).astype(jnp.bfloat16)
+    go.left(gain, small_sem.at[1])
+    go.left(squares.at[t], small_sem.at[3])
     go.finish()
-    for g in range(2):
-        for b in range(depth):
-            for side, when in sides:
-                pl.when(when)(lambda: att_copy(g, b, side).wait_send())
 
 
 def per_device_by_column(
@@ -600,7 +608,7 @@
     return pl.pallas_call(
         lambda *refs: column_kernel(depth, *refs),
         out_shape=(out, out),
-        in_specs=[hbm, smem, vmem, hbm, hbm, vmem, hbm, hbm, vmem],
+        in_specs=[hbm, smem, hbm, hbm, vmem, hbm, hbm],
         out_specs=(vmem, vmem),
         scratch_shapes=[
             bf16(depth, 2, span, half_width),
@@ -611,28 +619,33 @@
             bf16(PLANE, tokens, PAIR),
             bf16(2, depth, 2 * span, HEAD_SIZE),
             bf16(2, depth, tokens, PAIR),
-            f32(tokens, PLANE * width),
-            bf16(depth, span, PLANE * width),
-            bf16(depth, span, PLANE * width),
-            bf16(depth // 2, span, PLANE * width),
-            f32(2, span, HEAD_SIZE),
+            f32(depth // 2, PLANE, span, width),
+            bf16(depth, PLANE, span, width),
+            bf16(depth, PLANE, span, width),
+            bf16(depth // 2, PLANE, span, width),
+            f32(2, 8, span),
             bf16(depth, slab, PAIR),
             f32(depth, span, HEAD_SIZE),
             f32(depth, span, HEAD_SIZE),
             pltpu.VMEM((1, PLANE * tokens), jnp.int32),
             bf16(1, 2 * PAIR),
             bf16(2, HEAD_SIZE),
+            bf16(1, half_width),
+            bf16(4608, half_width),
             dma((8,)),
-            dma((224,)),
-            dma((depth, 2, PIECES)),
             dma((1,)),
-            dma((3, n_seq)),
-            dma((PLANE,)),
-            dma((PLANE,)),
+            dma((4,)),
+            dma((1,)),
+            dma((depth, PIECES)),
+            dma((depth,)),
+            dma((3, depth)),
+            dma((3,)),
+            dma((3,)),
+            dma((2,)),
+            dma((2,)),
             dma((2, depth, depth)),
-            dma((depth,)),
-            dma((depth // 2,)),
-            dma((1,)),
+            dma((depth, 2)),
+            dma((depth // 2, 2)),
         ],
         compiler_params=pltpu.CompilerParams(
             collective_id=0, has_side_effects=True, vmem_limit_bytes=60 * 1024 * 1024
@@ -641,13 +654,11 @@
     )(
         hidden_in,
         span_order,
-        norm_gain[None, :],
+        jnp.stack([norm_gain, bias_query, post_gain])[:, None, :],
         w_query,
-        bias_query[None, :],
         key_value_weight,
         bias_kv,
         w_out,
-        post_gain[None, :],
     )
 
 

time: 170 us -> 156 us (0.918); the launches traced: 170 us -> 154 us
  Pallas kernels: 164 us -> 149 us
    pallas_call x1, Pallas kernels: 164 us -> 149 us  [per_device_by_column(): pl.pallas_call(lambda *refs: column_kernel(depth, *refs), out_shape=(out,...]
    broadcast_in_dim x3 -> x1, local copies, waits for them, and re-layouts: 2.51 us -> 0.63 us  [per_device_by_column(): jnp.stack([norm_gain, bias_query, post_gain])[:, None, :]]
where the time goes in v2:
time: 156 us; the launch traced here: 154 us
  Pallas kernels  149 us (96%)
  local copies, waits for them, and re-layouts  4.75 us (3%)
    pallas_call x1, Pallas kernels, per_device_by_column(): pl.pallas_call(lambda *refs: column_kernel(depth, *refs), out_shape=(out,...  149 us
    unnamed x8, local copies, waits for them, and re-layouts  3.41 us

profile of v2, /device:TPU:8, one launch (start us, length us, event | category | flops | bytes accessed | tf_op | source)
XLA Modules:
  0.0 154.0 jit_solution(4816490866795817457)
XLA Ops:
  0.6 0.0 copy-start.1
  0.6 0.7 stack.12
  1.3 0.0 copy-done.1
  1.3 0.0 copy-start.2
  1.4 0.7 copy-done.2
  2.1 0.6 copy.11.refs_2_
  2.7 148.6 %sublayer.1 = (bf16[128,2048]{1,0:T(8,128)(2,1)}, bf16[128,2048]{1,0:T(8,128)(2,1)}) custom-call(bf16[128,2048]{1,0:T(8,128)(2,1)} %refs_0_.1, s32[16]{0:T(128)} %refs_1_.1, bf16[3,1,2048]{2,1,0:T(2,128)(2,1)} %copy.11.refs_2_, bf16[256,2048]{1,0:T(8,128)(2,1)} %refs_3_.1, bf16[256,2,512]{2,1,0:T(2,128)(2,1)} %refs_4_.1, bf16[2,512]{1,0:T(2,128)(2,1)} %refs_5_.1, ...), custom_call_target="tpu_custom_call" | custom-call | tf_op jit(solution)/shard_map/sublayer/pallas_call | solution.py:608
  151.3 0.0 copy-start
  151.3 1.9 %copy.14 = bf16[128,2048]{1,0:T(8,128)(2,1)} copy(bf16[128,2048]{1,0:T(8,128)(2,1)} %get-tuple-element.4) | data formatting | bytes 1048576
  153.3 0.0 copy-done
  153.3 0.8 copy.15
  (3 shorter events, 0.0 us)
Async XLA Ops:
  0.6 0.7 copy-start.1
  1.3 0.7 copy-start.2
  151.3 2.0 %copy-start = (bf16[128,2048]{1,0:T(8,128)(2,1)S(1)}, bf16[128,2048]{1,0:T(8,128)(2,1)}, u32[]{:S(2)}) copy-start(bf16[128,2048]{1,0:T(8,128)(2,1)} %get-tuple-element.5) | copy-start | bytes 1572868

commit v3 on v2

--- a/solution.py
+++ b/solution.py
@@ -226,12 +226,12 @@
 
 def column_kernel(
     depth,
-    hidden, order, vectors, wq, wkv, bias_kv, w_out,
-    attn_out, normed,
-    rows, full, gains, weights, outw, kvs, queries, att, acc, part, terms, others, squares,
-    kv_pieces, cos_t, sin_t, key_pos, bias_b, bias_p, post_gain, proxy,
+    hidden, order, gain, post_gain, bias_q, wq, wkv, bias_kv, w_out,
+    mixed_out, factor_out, post_out,
+    rows, full, gains, weights, outw, kvs, queries, att, part, terms, others, squares,
+    kv_pieces, cos_t, sin_t, key_pos, gain_rows, bias_b, bias_p, proxy,
     local_sem, send_sem, small_sem, relay_sem, rows_sem, rows_side_sem,
-    w_sem, w_across_sem, w_side_sem, out_sem, kv_sem, att_sem, term_sem, other_sem,
+    w_sem, w_across_sem, w_side_sem, out_end_sem, out_across_sem, out_side_sem, kv_sem, att_sem, term_sem, other_sem,
 ):
     s, t = lax.axis_index("seq"), lax.axis_index("tp")
     z, x, c = s // PLANE, s % PLANE // CORES, s % CORES
@@ -248,7 +248,6 @@
     pl.semaphore_wait(barrier, len(peers))
 
     go = Traffic(depth, z, send_sem, proxy, sibling)
-    gain, bias_q = vectors.at[0], vectors.at[1]
     edge = span // PIECES
 
     def bit(p):
@@ -262,22 +261,17 @@
         go.send(mine, landing, rows_sem.at[z, p], below, lambda k: k > 0)
     own = [
         pltpu.make_async_copy(hidden, rows.at[z, t], local_sem.at[0]),
-        pltpu.make_async_copy(gain, gains.at[t], local_sem.at[1]),
         pltpu.make_async_copy(
-            bias_q.at[:, pl.ds(pl.multiple_of(z * 2 * PAIR, PAIR), 2 * PAIR)], bias_b, local_sem.at[2]
+            bias_kv.at[:, pl.ds(pl.multiple_of(z * HEAD_SIZE, HEAD_SIZE), HEAD_SIZE)], bias_p, local_sem.at[1]
         ),
-        pltpu.make_async_copy(
-            bias_kv.at[:, pl.ds(pl.multiple_of(z * HEAD_SIZE, HEAD_SIZE), HEAD_SIZE)], bias_p, local_sem.at[3]
-        ),
-        pltpu.make_async_copy(w_out, outw.at[column], local_sem.at[4]),
-        pltpu.make_async_copy(vectors.at[2], post_gain, local_sem.at[7]),
+        pltpu.make_async_copy(w_out, outw.at[1, column], local_sem.at[2]),
     ]
 
     def q_piece(g, zt):
         return wq.at[:, pl.ds(pl.multiple_of(zt * 2 * PAIR + (g - 1) * PAIR, PAIR), PAIR)]
 
     for g in (1, 2):
-        own.append(pltpu.make_async_copy(q_piece(g, z), weights.at[g, s], local_sem.at[4 + g]))
+        own.append(pltpu.make_async_copy(q_piece(g, z), weights.at[g, s], local_sem.at[2 + g]))
     for copy in own:
         copy.start()
     for zt in range(depth):
@@ -288,8 +282,18 @@
         source = kv_pieces.at[z] if g == 0 else q_piece(g, z)
         go.send(source, weights.at[g, s], w_across_sem.at[g], across)
         go.send(source, weights.at[g, s], w_side_sem.at[g], sibling)
-    go.send(w_out, outw.at[column], out_sem.at[0], across)
-    go.send(w_out, outw.at[column], out_sem.at[1], sibling)
+    inner = lambda k: (k > 0) & (k < last)
+    outer = lambda k: (k == 0) | (k == last)
+    middle = inner(z)
+    go.send(w_out, outw.at[1, column], out_across_sem.at[1], across, inner)
+    go.send(w_out, outw.at[1, column], out_side_sem.at[1], sibling, inner)
+    own_end = jnp.where(z < depth // 2, 0, last)
+    gatherer = jnp.where(middle, last - z, jnp.where(z == 0, 1, last - 1))
+
+    def leave_columns(part_id):
+        place = pl.ds(part_id * (w_out.shape[0] // 2), w_out.shape[0] // 2)
+        landing = outw.at[0, column, place]
+        go.send(w_out.at[place], landing, out_end_sem.at[0], (at(gatherer, x, c), t), outer)
 
     def spread(stage, groups):
         for g in groups:
@@ -355,7 +359,7 @@
             factor = lax.rsqrt(total / (2 * half_width) + eps)
             for h in range(2):
                 full[zs, r, h * half_width : (h + 1) * half_width] = (
-                    halves[h] * factor * gains[h].astype(jnp.float32)
+                    halves[h] * factor * gain_rows[h]
                 ).astype(jnp.bfloat16)
             return carry
 
@@ -383,26 +387,37 @@
             )
     for copy in own:
         copy.wait()
+    gains[t] = gain[...]
     go.arrive(gains.at[1 - t], small_sem.at[0])
-
-    middle = jnp.logical_and(z > 0, z < last)
+    for h in range(2):
+        rows_of = gains[h].astype(jnp.float32)
+        for i in range(half_width // HEAD_SIZE):
+            gain_rows[h, :, i * HEAD_SIZE : (i + 1) * HEAD_SIZE] = rows_of[i : i + 1]
+    bias_b[...] = bias_q[...].astype(jnp.float32)
+    post_rows = post_gain[...].astype(jnp.float32)
+    for i in range(half_width // HEAD_SIZE):
+        post_out[:, i * HEAD_SIZE : (i + 1) * HEAD_SIZE] = post_rows[i : i + 1]
+
     pass_rows(1)
     spread(1, (0, 1, 2))
-    spread(3, (0,))
+    spread(3, (0, 1))
+    leave_columns(0)
     normalize(z)
     pass_rows(2)
     spread(2, (0, 1, 2))
+    leave_columns(1)
     for g in (0, 1, 2):
         take_weights(g, 1)
     normalize(z + 1 - 2 * lax.rem(z, 2))
     take_weights(0, 3)
+    take_weights(1, 3)
     go.left(rows.at[z, t], relay_sem.at[0], middle)
     pass_rows(3)
-    spread(3, (1, 2))
-    for g in (0, 1, 2):
+    spread(3, (2,))
+    for g in (0, 1):
         take_weights(g, 2)
     normalize(lax.rem(z + 2, depth))
-    take_weights(1, 3, (1, 2))
+    take_weights(2, 3, (1,))
     normalize(last - z)
     weights_across(0)
     weights_beside(0)
@@ -423,8 +438,17 @@
     kvs[column, :, HEAD_SIZE:] = (pair[:, HEAD_SIZE:] + bias_p[1:2, :].astype(jnp.float32)).astype(jnp.bfloat16)
     go.send(kvs.at[column], kvs.at[column], kv_sem.at[0], across)
     go.send(kvs.at[column], kvs.at[column], kv_sem.at[1], sibling)
-    take_weights(1, 3, (3,))
-    take_weights(2, 3)
+    take_weights(2, 2)
+    take_weights(2, 3, (2, 3))
+
+    @pl.when(middle)
+    def _():
+        block = outw.at[0, column]
+        go.arrive(block, out_end_sem.at[0])
+        go.remote(block, block, out_across_sem.at[0], across).start()
+        go.remote(block, block, out_side_sem.at[0], sibling).start()
+
+    go.count(outw.at[0, 0], inner, times=2)
 
     scale = math.log2(math.e) / math.sqrt(HEAD_SIZE)
 
@@ -432,8 +456,7 @@
         field = product(g)
         for i in range(2):
             cut = slice(i * HEAD_SIZE, (i + 1) * HEAD_SIZE)
-            wide = slice((g - 1) * PAIR + i * HEAD_SIZE, (g - 1) * PAIR + (i + 1) * HEAD_SIZE)
-            head = field[:, cut] + bias_b[:, wide].astype(jnp.float32)
+            head = field[:, cut] + bias_b[pl.ds(z * GROUP + (g - 1) * 2 + i, 1), :]
             turned = (rotate(head, cosine, sine) * scale).astype(jnp.bfloat16)
             queries[g - 1, :, i * span : (i + 1) * span, :] = turned.reshape(depth, span, HEAD_SIZE)
 
@@ -476,86 +499,97 @@
             att[g, z, place, :HEAD_SIZE] = result[:span]
             att[g, z, place, HEAD_SIZE:] = result[span:]
             block = att_piece(g, z, b)
-            pl.when(z < last)(lambda: go.remote(block, block, att_sem.at[g, z, b], above).start())
-            pl.when(z > 0)(lambda: go.remote(block, block, att_sem.at[g, z, b], below).start())
+            go.remote(block, block, att_sem.at[g, z, b], (at(gatherer, x, c), t)).start()
             return carry
 
         lax.fori_loop(0, depth, turn, 0)
-        go.count(att.at[g, 0], lambda k: k < last)
-        go.count(att.at[g, 0], lambda k: k > 0)
+        go.count(att.at[g, 0])
 
     attend(0)
     weights_across(2)
     weights_beside(2)
     make_queries(2)
+
+    def hand_on(g, i):
+        block, sem = att_piece(g, own_end, nth(i)), att_sem.at[g, own_end, nth(i)]
+        go.arrive(block, sem)
+        go.remote(block, block, sem, (at(last - z, x, c), t)).start()
+
+    @pl.when(middle)
+    def _():
+        for i in range(depth):
+            hand_on(0, i)
+
     attend(1)
-    outw_across = outw.at[(1 - x) * CORES + c]
-    go.arrive(outw_across, out_sem.at[0])
-    go.send(outw_across, outw_across, out_sem.at[1], sibling)
-    go.arrive(outw.at[pl.ds(0, CORES)], out_sem.at[1])
-
-    def pass_heads(g, b, distance):
-        def action(zs, where, target, more):
-            block, sem = att_piece(g, zs, b), att_sem.at[g, zs, b]
-            go.arrive(block, sem, where(z))
-            relay(block, sem, target, more)
-
-        chain(distance, action)
-
     halves = 2
     each = PLANE // halves
+    share = depth // 2
 
     def piece(ref, i, h):
         return ref.at[i, pl.ds(h * each, each)]
 
     def mix_block(b):
         place = pl.ds(pl.multiple_of(b * span, span), span)
-        for h in range(halves):
-            for m in range(h * each, (h + 1) * each):
-                total = None
-                for zs in range(depth):
-                    for g in range(2):
-                        first = zs * 2 * PAIR + g * PAIR
-                        term = jnp.dot(
-                            att[g, zs, place, :], outw[m, first : first + PAIR, :], preferred_element_type=jnp.float32
-                        )
-                        total = term if total is None else total + term
-                value = total.astype(jnp.bfloat16)
-
-                @pl.when(b == z)
-                def _():
-                    terms[z, m] = value
+        for e, owner in ((0, own_end), (1, z)):
+            for h in range(halves):
+                for m in range(h * each, (h + 1) * each):
+                    total = None
+                    for zs in range(depth):
+                        for g in range(2):
+                            first = zs * 2 * PAIR + g * PAIR
+                            term = jnp.dot(
+                                att[g, zs, place, :],
+                                outw[e, m, first : first + PAIR, :],
+                                preferred_element_type=jnp.float32,
+                            )
+                            total = term if total is None else total + term
+                    value = total.astype(jnp.bfloat16)
+
+                    @pl.when(b == z)
+                    def _():
+                        terms[owner, m] = value
+
+                    @pl.when(b != z)
+                    def _():
+                        part[e, b, m] = value
 
                 @pl.when(b != z)
                 def _():
-                    part[b, m] = value
-
-            @pl.when(b != z)
-            def _():
-                go.remote(piece(part, b, h), piece(terms, z, h), term_sem.at[z, h], (at(b, x, c), t)).start()
-
-    share = depth // 2
-
-    def settle():
-        for zs in (1, 2, 0, 3):
-            for h in range(halves):
-                block = piece(terms, zs, h)
-                go.arrive(block, term_sem.at[zs, h], z != zs)
-                landing, sem = piece(others, zs % share, h), other_sem.at[zs % share, h]
-                go.send(block, landing, sem, other, also=t != zs // share)
-
-    for g in range(2):
+                    source = piece(part.at[e], b, h)
+                    go.remote(source, piece(terms, owner, h), term_sem.at[owner, h], (at(b, x, c), t)).start()
+
+    @pl.when(middle)
+    def _():
+        def side_columns(e):
+            block = outw.at[e, (1 - x) * CORES + c]
+            go.arrive(block, out_across_sem.at[e])
+            go.remote(block, block, out_side_sem.at[e], sibling).start()
+
+        side_columns(1)
         for i in range(depth):
-            pass_heads(g, nth(i), 1)
-    for i in range(depth):
-        for g in range(2):
-            pass_heads(g, nth(i), 2)
-    for i in range(depth):
-        for g in range(2):
-            pass_heads(g, nth(i), 3)
-        mix_block(nth(i))
-    settle()
-    go.count(part.at[0], times=depth - 1)
+            hand_on(1, i)
+        side_columns(0)
+        for e in (1, 0):
+            go.arrive(outw.at[e, pl.ds(0, CORES)], out_side_sem.at[e])
+        for i in range(depth):
+            for zs in (last - z, last - own_end):
+                for g in range(2):
+                    go.arrive(att_piece(g, zs, nth(i)), att_sem.at[g, zs, nth(i)])
+            mix_block(nth(i))
+
+    go.count(outw.at[0, 0], inner, times=2)
+    go.count(att.at[:, 0], inner)
+    go.count(part.at[0, 0], inner, times=2 * (depth - 1))
+
+    near = jnp.where(z < share, 0, share)
+    for e in range(2):
+        for h in range(halves):
+            for first in (near, share - near):
+                maker = jnp.where(first == 0, 1, last - 1)
+                index = jnp.where(first == 0, e, 1 - e)
+                block = piece(terms, first + index, h)
+                go.arrive(block, term_sem.at[first + index, h], z != maker)
+                go.send(block, piece(others, index, h), other_sem.at[index, h], other, also=t != first // share)
     go.count(others.at[0], times=share)
 
     width = w_out.shape[1]
@@ -566,18 +600,14 @@
             go.arrive(piece(others, j, m // each), other_sem.at[j, m // each])
         cut = slice((j * PLANE + m) * width, (j * PLANE + m + 1) * width)
         mixed = terms[t * share + j, m].astype(jnp.float32) + others[j, m].astype(jnp.float32)
-        attn_out[:, cut] = mixed.astype(jnp.bfloat16)
+        mixed_out[:, cut] = mixed
         stream = rows[z, t, :, cut].astype(jnp.float32) + mixed
-        acc[j, m] = stream
         sums = sums + jnp.sum(stream * stream, axis=1, keepdims=True)
     squares[t] = jnp.broadcast_to(sums, (span, span)).T[:8]
     go.send(squares.at[t], squares.at[t], small_sem.at[2], other, sem=small_sem.at[3])
     go.arrive(squares.at[1 - t], small_sem.at[2])
-    total = jnp.broadcast_to((squares[0] + squares[1])[:1], (span, span)).T
-    factor = lax.rsqrt(total / (2 * half_width) + eps)[:, :1]
-    for j, m in pieces:
-        cut = slice((j * PLANE + m) * width, (j * PLANE + m + 1) * width)
-        normed[:, cut] = (acc[j, m] * factor * post_gain[:, cut].astype(jnp.float32)).astype(jnp.bfloat16)
+    total = (squares[0] + squares[1])[:1]
+    factor_out[...] = lax.rsqrt(total / (2 * half_width) + eps)
     go.left(gain, small_sem.at[1])
     go.left(squares.at[t], small_sem.at[3])
     go.finish()
@@ -601,26 +631,25 @@
     tokens = depth * span
     vmem, hbm, smem = (pl.BlockSpec(memory_space=m) for m in (pltpu.VMEM, pl.ANY, pltpu.SMEM))
     dma = pltpu.SemaphoreType.DMA
-    out = jax.ShapeDtypeStruct((span, half_width), jnp.bfloat16)
     bf16 = lambda *shape: pltpu.VMEM(shape, jnp.bfloat16)
     f32 = lambda *shape: pltpu.VMEM(shape, jnp.float32)
     width = w_out.shape[1]
-    return pl.pallas_call(
+    f32_out = lambda *shape: jax.ShapeDtypeStruct(shape, jnp.float32)
+    mixed, factor, post = pl.pallas_call(
         lambda *refs: column_kernel(depth, *refs),
-        out_shape=(out, out),
-        in_specs=[hbm, smem, hbm, hbm, vmem, hbm, hbm],
-        out_specs=(vmem, vmem),
+        out_shape=(f32_out(span, half_width), f32_out(1, span), f32_out(1, half_width)),
+        in_specs=[hbm, smem, vmem, vmem, vmem, hbm, vmem, hbm, hbm],
+        out_specs=(vmem, vmem, vmem),
         scratch_shapes=[
             bf16(depth, 2, span, half_width),
             bf16(depth, span, 2 * half_width),
-            bf16(2, 1, half_width),
+            bf16(2, half_width // HEAD_SIZE, HEAD_SIZE),
             bf16(3, n_seq, slab, PAIR),
-            bf16(PLANE, w_out.shape[0], width),
+            bf16(2, PLANE, w_out.shape[0], width),
             bf16(PLANE, tokens, PAIR),
             bf16(2, depth, 2 * span, HEAD_SIZE),
             bf16(2, depth, tokens, PAIR),
-            f32(depth // 2, PLANE, span, width),
-            bf16(depth, PLANE, span, width),
+            bf16(2, depth, PLANE, span, width),
             bf16(depth, PLANE, span, width),
             bf16(depth // 2, PLANE, span, width),
             f32(2, 8, span),
@@ -628,11 +657,11 @@
             f32(depth, span, HEAD_SIZE),
             f32(depth, span, HEAD_SIZE),
             pltpu.VMEM((1, PLANE * tokens), jnp.int32),
-            bf16(1, 2 * PAIR),
+            f32(2, 1, half_width),
+            f32(half_width // HEAD_SIZE, HEAD_SIZE),
             bf16(2, HEAD_SIZE),
-            bf16(1, half_width),
-            bf16(4608, half_width),
-            dma((8,)),
+            bf16(5120, half_width),
+            dma((5,)),
             dma((1,)),
             dma((4,)),
             dma((1,)),
@@ -641,6 +670,8 @@
             dma((3, depth)),
             dma((3,)),
             dma((3,)),
+            dma((1,)),
+            dma((2,)),
             dma((2,)),
             dma((2,)),
             dma((2, depth, depth)),
@@ -654,12 +685,17 @@
     )(
         hidden_in,
         span_order,
-        jnp.stack([norm_gain, bias_query, post_gain])[:, None, :],
+        norm_gain.reshape(-1, HEAD_SIZE),
+        post_gain.reshape(-1, HEAD_SIZE),
+        bias_query.reshape(-1, HEAD_SIZE),
         w_query,
         key_value_weight,
         bias_kv,
         w_out,
     )
+    stream = hidden_in.astype(jnp.float32) + mixed
+    normed = (stream * factor.reshape(span, 1) * post).astype(jnp.bfloat16)
+    return (mixed.astype(jnp.bfloat16), normed)
 
 
 def per_device(*args):

time: 156 us -> 146 us (0.936)
  the two profiles are of different devices: /device:TPU:8 before, /device:TPU:20 now
where the time goes in v3:
time: 146 us; the launch traced here: 145 us
  Pallas kernels  141 us (97%)
  other arithmetic  2.78 us (2%)
    pallas_call x1, Pallas kernels, per_device_by_column(): pl.pallas_call(lambda *refs: column_kernel(depth, *refs), out_shape=(f32_...  141 us

profile of v3, /device:TPU:20, one launch (start us, length us, event | category | flops | bytes accessed | tf_op | source)
XLA Modules:
  0.0 145.3 jit_solution(17257347567717074026)
XLA Ops:
  0.6 0.0 copy-start
  0.6 141.2 %sublayer.1 = (f32[128,2048]{1,0:T(8,128)}, f32[1,128]{1,0:T(1,128)}, f32[1,2048]{1,0:T(1,128)}) custom-call(bf16[128,2048]{1,0:T(8,128)(2,1)} %refs_0_.1, s32[16]{0:T(128)} %refs_1_.1, bf16[16,128]{1,0:T(8,128)(2,1)} %bitcast.6, bf16[16,128]{1,0:T(8,128)(2,1)} %bitcast.7, bf16[16,128]{1,0:T(8,128)(2,1)} %bitcast.8, bf16[256,2048]{1,0:T(8,128)(2,1)} %refs_5_.1, ...), custom_call_target="tpu_custom_call" | custom-call | tf_op jit(solution)/shard_map/sublayer/pallas_call | solution.py:638
  141.9 0.0 copy-start.1
  141.9 0.0 copy-start.2
  141.9 0.0 copy-done
  141.9 0.7 copy-done.1
  142.6 0.0 copy-done.2
  142.6 2.8 %multiply_convert_fusion = (bf16[128,2048]{1,0:T(8,128)(2,1)}, bf16[128,2048]{1,0:T(8,128)(2,1)}) fusion(f32[128,2048]{1,0:T(8,128)} %get-tuple-element.5, bf16[128,2048]{1,0:T(8,128)(2,1)S(1)} %copy-done, f32[2048]{0:T(1024)S(1)} %bitcast.5, f32[128]{0:T(128)S(1)} %bitcast.9), kind=kLoop, calls=%fused_computation | loop fusion | flops 1572864 | bytes 2630144 | tf_op jit(solution)/shard_map/convert_element_type | solution.py:697
Async XLA Ops:
  0.6 141.2 %copy-start = (bf16[128,2048]{1,0:T(8,128)(2,1)S(1)}, bf16[128,2048]{1,0:T(8,128)(2,1)}, u32[]{:S(2)}) copy-start(bf16[128,2048]{1,0:T(8,128)(2,1)} %refs_0_.1) | copy-start | bytes 1572868
  141.9 0.7 copy-start.1
  141.9 0.7 copy-start.2

commit v4 on v3

--- a/solution.py
+++ b/solution.py
@@ -229,7 +229,7 @@
     hidden, order, gain, post_gain, bias_q, wq, wkv, bias_kv, w_out,
     mixed_out, factor_out, post_out,
     rows, full, gains, weights, outw, kvs, queries, att, part, terms, others, squares,
-    kv_pieces, cos_t, sin_t, key_pos, gain_rows, bias_b, bias_p, proxy,
+    kv_pieces, cos_t, sin_t, key_pos, gain_rows, bias_b, bias_p, mixed_rows, proxy,
     local_sem, send_sem, small_sem, relay_sem, rows_sem, rows_side_sem,
     w_sem, w_across_sem, w_side_sem, out_end_sem, out_across_sem, out_side_sem, kv_sem, att_sem, term_sem, other_sem,
 ):
@@ -400,24 +400,23 @@
 
     pass_rows(1)
     spread(1, (0, 1, 2))
-    spread(3, (0, 1))
+    spread(3, (0,))
     leave_columns(0)
     normalize(z)
     pass_rows(2)
     spread(2, (0, 1, 2))
-    leave_columns(1)
     for g in (0, 1, 2):
         take_weights(g, 1)
     normalize(z + 1 - 2 * lax.rem(z, 2))
     take_weights(0, 3)
-    take_weights(1, 3)
+    take_weights(0, 2)
     go.left(rows.at[z, t], relay_sem.at[0], middle)
     pass_rows(3)
-    spread(3, (2,))
-    for g in (0, 1):
-        take_weights(g, 2)
+    spread(3, (1,))
+    leave_columns(1)
+    take_weights(1, 2)
     normalize(lax.rem(z + 2, depth))
-    take_weights(2, 3, (1,))
+    take_weights(1, 3, (1, 2))
     normalize(last - z)
     weights_across(0)
     weights_beside(0)
@@ -438,17 +437,10 @@
     kvs[column, :, HEAD_SIZE:] = (pair[:, HEAD_SIZE:] + bias_p[1:2, :].astype(jnp.float32)).astype(jnp.bfloat16)
     go.send(kvs.at[column], kvs.at[column], kv_sem.at[0], across)
     go.send(kvs.at[column], kvs.at[column], kv_sem.at[1], sibling)
+    spread(3, (2,))
     take_weights(2, 2)
-    take_weights(2, 3, (2, 3))
-
-    @pl.when(middle)
-    def _():
-        block = outw.at[0, column]
-        go.arrive(block, out_end_sem.at[0])
-        go.remote(block, block, out_across_sem.at[0], across).start()
-        go.remote(block, block, out_side_sem.at[0], sibling).start()
-
-    go.count(outw.at[0, 0], inner, times=2)
+    take_weights(1, 3, (3,))
+    take_weights(2, 3)
 
     scale = math.log2(math.e) / math.sqrt(HEAD_SIZE)
 
@@ -474,7 +466,7 @@
     def nth(i):
         return jnp.where(i == 0, 0, jnp.where(i == 1, last, jnp.where(i == 2, 1 + c, 2 - c)))
 
-    def attend(g):
+    def attend(g, first, end):
         def turn(i, carry):
             b = nth(i)
             scores = lax.dot_general(
@@ -483,8 +475,8 @@
                 (((1,), (1,)), ((), ())),
                 preferred_element_type=jnp.float32,
             )
-            first = order[b * PLANE + column] * span
-            query_pos = first + lax.rem(lax.broadcasted_iota(jnp.int32, (2 * span, 1), 0), span)
+            start = order[b * PLANE + column] * span
+            query_pos = start + lax.rem(lax.broadcasted_iota(jnp.int32, (2 * span, 1), 0), span)
             scores = jnp.where(key_pos[...] <= query_pos, scores, -jnp.inf)
             peak = jnp.max(scores, axis=1, keepdims=True)
             shares = jnp.exp2(scores - peak)
@@ -502,25 +494,29 @@
             go.remote(block, block, att_sem.at[g, z, b], (at(gatherer, x, c), t)).start()
             return carry
 
-        lax.fori_loop(0, depth, turn, 0)
-        go.count(att.at[g, 0])
-
-    attend(0)
+        lax.fori_loop(first, end, turn, 0)
+
+    attend(0, 0, depth)
+
+    @pl.when(middle)
+    def _():
+        block = outw.at[0, column]
+        go.arrive(block, out_end_sem.at[0])
+        go.remote(block, block, out_across_sem.at[0], across).start()
+        go.remote(block, block, out_side_sem.at[0], sibling).start()
+
+    go.count(outw.at[0, 0], inner, times=2)
     weights_across(2)
     weights_beside(2)
     make_queries(2)
+    attend(1, 0, depth)
+    go.count(att.at[0, 0], times=2)
 
     def hand_on(g, i):
         block, sem = att_piece(g, own_end, nth(i)), att_sem.at[g, own_end, nth(i)]
         go.arrive(block, sem)
         go.remote(block, block, sem, (at(last - z, x, c), t)).start()
 
-    @pl.when(middle)
-    def _():
-        for i in range(depth):
-            hand_on(0, i)
-
-    attend(1)
     halves = 2
     each = PLANE // halves
     share = depth // 2
@@ -528,35 +524,35 @@
     def piece(ref, i, h):
         return ref.at[i, pl.ds(h * each, each)]
 
-    def mix_block(b):
+    def mix_block(e, b):
         place = pl.ds(pl.multiple_of(b * span, span), span)
-        for e, owner in ((0, own_end), (1, z)):
-            for h in range(halves):
-                for m in range(h * each, (h + 1) * each):
-                    total = None
-                    for zs in range(depth):
-                        for g in range(2):
-                            first = zs * 2 * PAIR + g * PAIR
-                            term = jnp.dot(
-                                att[g, zs, place, :],
-                                outw[e, m, first : first + PAIR, :],
-                                preferred_element_type=jnp.float32,
-                            )
-                            total = term if total is None else total + term
-                    value = total.astype(jnp.bfloat16)
-
-                    @pl.when(b == z)
-                    def _():
-                        terms[owner, m] = value
-
-                    @pl.when(b != z)
-                    def _():
-                        part[e, b, m] = value
+        owner = own_end if e == 0 else z
+        for h in range(halves):
+            for m in range(h * each, (h + 1) * each):
+                total = None
+                for zs in range(depth):
+                    for g in range(2):
+                        first = zs * 2 * PAIR + g * PAIR
+                        term = jnp.dot(
+                            att[g, zs, place, :],
+                            outw[e, m, first : first + PAIR, :],
+                            preferred_element_type=jnp.float32,
+                        )
+                        total = term if total is None else total + term
+                value = total.astype(jnp.bfloat16)
+
+                @pl.when(b == z)
+                def _():
+                    terms[owner, m] = value
 
                 @pl.when(b != z)
                 def _():
-                    source = piece(part.at[e], b, h)
-                    go.remote(source, piece(terms, owner, h), term_sem.at[owner, h], (at(b, x, c), t)).start()
+                    part[e, b, m] = value
+
+            @pl.when(b != z)
+            def _():
+                source = piece(part.at[e], b, h)
+                go.remote(source, piece(terms, owner, h), term_sem.at[owner, h], (at(b, x, c), t)).start()
 
     @pl.when(middle)
     def _():
@@ -566,23 +562,27 @@
             go.remote(block, block, out_side_sem.at[e], sibling).start()
 
         side_columns(1)
-        for i in range(depth):
-            hand_on(1, i)
-        side_columns(0)
-        for e in (1, 0):
-            go.arrive(outw.at[e, pl.ds(0, CORES)], out_side_sem.at[e])
+        for g in range(2):
+            for i in range(depth):
+                hand_on(g, i)
+        go.arrive(outw.at[1, pl.ds(0, CORES)], out_side_sem.at[1])
         for i in range(depth):
             for zs in (last - z, last - own_end):
                 for g in range(2):
                     go.arrive(att_piece(g, zs, nth(i)), att_sem.at[g, zs, nth(i)])
-            mix_block(nth(i))
+            mix_block(1, nth(i))
+            if i == 1:
+                side_columns(0)
+        go.arrive(outw.at[0, pl.ds(0, CORES)], out_side_sem.at[0])
+        for i in range(depth):
+            mix_block(0, nth(i))
 
     go.count(outw.at[0, 0], inner, times=2)
     go.count(att.at[:, 0], inner)
     go.count(part.at[0, 0], inner, times=2 * (depth - 1))
 
     near = jnp.where(z < share, 0, share)
-    for e in range(2):
+    for e in (1, 0):
         for h in range(halves):
             for first in (near, share - near):
                 maker = jnp.where(first == 0, 1, last - 1)
@@ -600,14 +600,17 @@
             go.arrive(piece(others, j, m // each), other_sem.at[j, m // each])
         cut = slice((j * PLANE + m) * width, (j * PLANE + m + 1) * width)
         mixed = terms[t * share + j, m].astype(jnp.float32) + others[j, m].astype(jnp.float32)
-        mixed_out[:, cut] = mixed
+        mixed_rows[:, cut] = mixed
         stream = rows[z, t, :, cut].astype(jnp.float32) + mixed
         sums = sums + jnp.sum(stream * stream, axis=1, keepdims=True)
+    write = pltpu.make_async_copy(mixed_rows, mixed_out, local_sem.at[0])
+    write.start()
     squares[t] = jnp.broadcast_to(sums, (span, span)).T[:8]
     go.send(squares.at[t], squares.at[t], small_sem.at[2], other, sem=small_sem.at[3])
     go.arrive(squares.at[1 - t], small_sem.at[2])
     total = (squares[0] + squares[1])[:1]
     factor_out[...] = lax.rsqrt(total / (2 * half_width) + eps)
+    write.wait()
     go.left(gain, small_sem.at[1])
     go.left(squares.at[t], small_sem.at[3])
     go.finish()
@@ -639,7 +642,7 @@
         lambda *refs: column_kernel(depth, *refs),
         out_shape=(f32_out(span, half_width), f32_out(1, span), f32_out(1, half_width)),
         in_specs=[hbm, smem, vmem, vmem, vmem, hbm, vmem, hbm, hbm],
-        out_specs=(vmem, vmem, vmem),
+        out_specs=(hbm, vmem, vmem),
         scratch_shapes=[
             bf16(depth, 2, span, half_width),
             bf16(depth, span, 2 * half_width),
@@ -660,6 +663,7 @@
             f32(2, 1, half_width),
             f32(half_width // HEAD_SIZE, HEAD_SIZE),
             bf16(2, HEAD_SIZE),
+            f32(span, half_width),
             bf16(5120, half_width),
             dma((5,)),
             dma((1,)),

time: 146 us -> 134 us (0.918)
  the two profiles are of different devices: /device:TPU:20 before, /device:TPU:8 now
where the time goes in v4:
time: 134 us; the launch traced here: 133 us
  Pallas kernels  129 us (96%)
  other arithmetic  2.78 us (2%)
    pallas_call x1, Pallas kernels, per_device_by_column(): pl.pallas_call(lambda *refs: column_kernel(depth, *refs), out_shape=(f32_...  129 us
    convert_element_type x1, other arithmetic, per_device_by_column(): normed = (stream * factor.reshape(span, 1) * post).astype(jnp.bfloat16)  2.78 us

profile of v4, /device:TPU:8, one launch (start us, length us, event | category | flops | bytes accessed | tf_op | source)
XLA Modules:
  0.0 133.3 jit_solution(7517617253795229444)
XLA Ops:
  0.6 0.0 copy-start
  0.6 129.2 %sublayer.1 = (f32[128,2048]{1,0:T(8,128)}, f32[1,128]{1,0:T(1,128)}, f32[1,2048]{1,0:T(1,128)}) custom-call(bf16[128,2048]{1,0:T(8,128)(2,1)} %refs_0_.1, s32[16]{0:T(128)} %refs_1_.1, bf16[16,128]{1,0:T(8,128)(2,1)} %bitcast.6, bf16[16,128]{1,0:T(8,128)(2,1)} %bitcast.7, bf16[16,128]{1,0:T(8,128)(2,1)} %bitcast.8, bf16[256,2048]{1,0:T(8,128)(2,1)} %refs_5_.1, ...), custom_call_target="tpu_custom_call" | custom-call | tf_op jit(solution)/shard_map/sublayer/pallas_call | solution.py:641
  129.9 0.0 copy-start.1
  129.9 0.0 copy-start.2
  129.9 0.0 copy-done
  129.9 0.7 copy-done.1
  130.5 0.0 copy-done.2
  130.6 2.8 %multiply_convert_fusion = (bf16[128,2048]{1,0:T(8,128)(2,1)}, bf16[128,2048]{1,0:T(8,128)(2,1)}) fusion(f32[128,2048]{1,0:T(8,128)} %get-tuple-element.5, bf16[128,2048]{1,0:T(8,128)(2,1)S(1)} %copy-done, f32[2048]{0:T(1024)S(1)} %bitcast.5, f32[128]{0:T(128)S(1)} %bitcast.9), kind=kLoop, calls=%fused_computation | loop fusion | flops 1572864 | bytes 2630144 | tf_op jit(solution)/shard_map/convert_element_type | solution.py:701
Async XLA Ops:
  0.6 129.2 %copy-start = (bf16[128,2048]{1,0:T(8,128)(2,1)S(1)}, bf16[128,2048]{1,0:T(8,128)(2,1)}, u32[]{:S(2)}) copy-start(bf16[128,2048]{1,0:T(8,128)(2,1)} %refs_0_.1) | copy-start | bytes 1572868
  129.9 0.7 copy-start.1
  129.9 0.7 copy-start.2

commit v5 on v4

--- a/solution.py
+++ b/solution.py
@@ -175,13 +175,13 @@
 class Traffic:
     def __init__(self, depth, z, sem, proxy, peer):
         self.z, self.sem, self.proxy, self.peer = z, sem, proxy, peer
-        self.rows = [0] * depth
+        self.rows, self.epoch = [[0] * depth, [0] * depth], 0
 
     def remote(self, source, landing, arrival, target, sem=None):
         return pltpu.make_async_remote_copy(
             src_ref=source,
             dst_ref=landing,
-            send_sem=self.sem.at[0] if sem is None else sem,
+            send_sem=self.sem.at[self.epoch] if sem is None else sem,
             recv_sem=arrival,
             device_id=target,
             device_id_type=MESH,
@@ -189,9 +189,10 @@
 
     def count(self, ref, where=None, times=1):
         size = math.prod(ref.shape) * times // self.proxy.shape[1]
-        for k in range(len(self.rows)):
+        rows = self.rows[self.epoch]
+        for k in range(len(rows)):
             if where is None or where(k):
-                self.rows[k] += size
+                rows[k] += size
 
     def send(self, source, landing, arrival, target, where=None, also=None, sem=None):
         when = None if where is None else where(self.z)
@@ -208,9 +209,10 @@
         guarded(when, lambda: self.remote(source, source, sem, self.peer, sem).wait_send())
 
     def finish(self):
-        for k, size in enumerate(self.rows):
-            block = self.proxy.at[pl.ds(0, size)]
-            self.left(block, self.sem.at[0], self.z == k)
+        for epoch, rows in enumerate(self.rows):
+            for k, size in enumerate(rows):
+                block = self.proxy.at[pl.ds(0, size)]
+                self.left(block, self.sem.at[epoch], self.z == k)
 
 
 def guarded(when, action):
@@ -229,7 +231,7 @@
     hidden, order, gain, post_gain, bias_q, wq, wkv, bias_kv, w_out,
     mixed_out, factor_out, post_out,
     rows, full, gains, weights, outw, kvs, queries, att, part, terms, others, squares,
-    kv_pieces, cos_t, sin_t, key_pos, gain_rows, bias_b, bias_p, mixed_rows, proxy,
+    kv_pieces, cos_t, sin_t, key_pos, gain_rows, bias_b, bias_p, early, premixed, mixed_rows, proxy,
     local_sem, send_sem, small_sem, relay_sem, rows_sem, rows_side_sem,
     w_sem, w_across_sem, w_side_sem, out_end_sem, out_across_sem, out_side_sem, kv_sem, att_sem, term_sem, other_sem,
 ):
@@ -237,6 +239,7 @@
     z, x, c = s // PLANE, s % PLANE // CORES, s % CORES
     last = depth - 1
     span, half_width = hidden.shape
+    slab = wq.shape[0]
     column = x * CORES + c
     sibling, across, other = (at(z, x, 1 - c), t), (at(z, 1 - x, c), t), (s, 1 - t)
     above, below = (at(jnp.minimum(z + 1, last), x, c), t), (at(jnp.maximum(z - 1, 0), x, c), t)
@@ -271,17 +274,17 @@
         return wq.at[:, pl.ds(pl.multiple_of(zt * 2 * PAIR + (g - 1) * PAIR, PAIR), PAIR)]
 
     for g in (1, 2):
-        own.append(pltpu.make_async_copy(q_piece(g, z), weights.at[g, s], local_sem.at[2 + g]))
+        own.append(pltpu.make_async_copy(q_piece(g, z), weights.at[g, c, s // CORES], local_sem.at[2 + g]))
     for copy in own:
         copy.start()
     for zt in range(depth):
         for i in range(2):
             kv_pieces[zt, :, i * HEAD_SIZE : (i + 1) * HEAD_SIZE] = wkv[:, i, zt * HEAD_SIZE : (zt + 1) * HEAD_SIZE]
-    weights[0, s] = kv_pieces[z]
+    weights[0, c, s // CORES] = kv_pieces[z]
     for g in (0, 1, 2):
         source = kv_pieces.at[z] if g == 0 else q_piece(g, z)
-        go.send(source, weights.at[g, s], w_across_sem.at[g], across)
-        go.send(source, weights.at[g, s], w_side_sem.at[g], sibling)
+        go.send(source, weights.at[g, c, s // CORES], w_across_sem.at[g], across)
+        go.send(source, weights.at[g, c, s // CORES], w_side_sem.at[g], sibling)
     inner = lambda k: (k > 0) & (k < last)
     outer = lambda k: (k == 0) | (k == last)
     middle = inner(z)
@@ -299,13 +302,13 @@
         for g in groups:
             for zt, where in ((stage, lambda k: k < stage), (last - stage, lambda k: k > last - stage)):
                 source = kv_pieces.at[zt] if g == 0 else q_piece(g, zt)
-                go.send(source, weights.at[g, s], w_sem.at[g, z], (at(zt, x, c), t), where)
+                go.send(source, weights.at[g, c, s // CORES], w_sem.at[g, z], (at(zt, x, c), t), where)
 
     def take_weights(g, stage, distances=None):
         for distance in distances or range(1, stage + 1):
             for sign, goal in ((-1, stage), (1, last - stage)):
                 zs = jnp.clip(z + sign * distance, 0, last)
-                block = weights.at[g, at(zs, x, c)]
+                block = weights.at[g, c, zs * CORES + x]
                 go.arrive(block, w_sem.at[g, zs], z == goal)
                 go.send(block, block, w_across_sem.at[g], across, lambda k: k == goal)
                 go.send(block, block, w_side_sem.at[g], sibling, lambda k: k == goal)
@@ -341,13 +344,13 @@
             chain(distance, action)
 
     def weights_across(g):
-        go.arrive(weights.at[g, pl.ds(0, depth)], w_across_sem.at[g])
+        go.arrive(weights.at[g, c, pl.ds(0, depth)], w_across_sem.at[g])
         for zs in range(depth):
-            block = weights.at[g, at(zs, 1 - x, c)]
+            block = weights.at[g, c, zs * CORES + 1 - x]
             go.send(block, block, w_side_sem.at[g], sibling)
 
     def weights_beside(g):
-        go.arrive(weights.at[g, pl.ds(0, depth * CORES)], w_side_sem.at[g])
+        go.arrive(weights.at[g, 1 - c], w_side_sem.at[g])
 
     def normalize(zs):
         go.arrive(rows.at[zs, 1 - t], rows_side_sem.at[zs])
@@ -358,9 +361,10 @@
             total = sum(jnp.sum(a * a, axis=1, keepdims=True) for a in halves)
             factor = lax.rsqrt(total / (2 * half_width) + eps)
             for h in range(2):
-                full[zs, r, h * half_width : (h + 1) * half_width] = (
-                    halves[h] * factor * gain_rows[h]
-                ).astype(jnp.bfloat16)
+                value = (halves[h] * factor * gain_rows[h]).astype(jnp.bfloat16)
+                for i in range(half_width // slab):
+                    j, core = divmod(h * (half_width // slab) + i, CORES)
+                    full[core, zs, r, j * slab : (j + 1) * slab] = value[:, i * slab : (i + 1) * slab]
             return carry
 
         lax.fori_loop(0, span // 16, strip, 0)
@@ -419,33 +423,41 @@
     take_weights(1, 3, (1, 2))
     normalize(last - z)
     weights_across(0)
-    weights_beside(0)
 
     tokens = depth * span
 
-    def product(g):
+    def kv_block(i):
+        return kvs.at[i]
+
+    def product(g, core):
         return jnp.dot(
-            full[...].reshape(tokens, 2 * half_width),
-            weights[g].reshape(2 * half_width, PAIR),
+            full[core].reshape(tokens, half_width),
+            weights[g, core].reshape(half_width, PAIR),
             preferred_element_type=jnp.float32,
         )
 
+    def whole_product(g):
+        early[...] = product(g, c)
+        weights_beside(g)
+        return early[...] + product(g, 1 - c)
+
     cosine, sine = cos_t[...].reshape(tokens, HEAD_SIZE), sin_t[...].reshape(tokens, HEAD_SIZE)
-    pair = product(0)
+    pair = whole_product(0)
     keys = pair[:, :HEAD_SIZE] + bias_p[0:1, :].astype(jnp.float32)
     kvs[column, :, :HEAD_SIZE] = rotate(keys, cosine, sine).astype(jnp.bfloat16)
     kvs[column, :, HEAD_SIZE:] = (pair[:, HEAD_SIZE:] + bias_p[1:2, :].astype(jnp.float32)).astype(jnp.bfloat16)
-    go.send(kvs.at[column], kvs.at[column], kv_sem.at[0], across)
-    go.send(kvs.at[column], kvs.at[column], kv_sem.at[1], sibling)
+    go.send(kv_block(column), kv_block(column), kv_sem.at[0], across)
+    go.send(kv_block(column), kv_block(column), kv_sem.at[1], sibling)
     spread(3, (2,))
     take_weights(2, 2)
     take_weights(1, 3, (3,))
     take_weights(2, 3)
 
+    go.epoch = 1
     scale = math.log2(math.e) / math.sqrt(HEAD_SIZE)
 
     def make_queries(g):
-        field = product(g)
+        field = whole_product(g)
         for i in range(2):
             cut = slice(i * HEAD_SIZE, (i + 1) * HEAD_SIZE)
             head = field[:, cut] + bias_b[pl.ds(z * GROUP + (g - 1) * 2 + i, 1), :]
@@ -453,9 +465,8 @@
             queries[g - 1, :, i * span : (i + 1) * span, :] = turned.reshape(depth, span, HEAD_SIZE)
 
     weights_across(1)
-    weights_beside(1)
     make_queries(1)
-    kv_across = kvs.at[(1 - x) * CORES + c]
+    kv_across = kv_block((1 - x) * CORES + c)
     go.arrive(kv_across, kv_sem.at[0])
     go.send(kv_across, kv_across, kv_sem.at[1], sibling)
     go.arrive(kvs.at[pl.ds(0, CORES)], kv_sem.at[1])
@@ -507,7 +518,6 @@
 
     go.count(outw.at[0, 0], inner, times=2)
     weights_across(2)
-    weights_beside(2)
     make_queries(2)
     attend(1, 0, depth)
     go.count(att.at[0, 0], times=2)
@@ -517,28 +527,29 @@
         go.arrive(block, sem)
         go.remote(block, block, sem, (at(last - z, x, c), t)).start()
 
-    halves = 2
+    halves = PLANE
     each = PLANE // halves
     share = depth // 2
 
     def piece(ref, i, h):
         return ref.at[i, pl.ds(h * each, each)]
+
+    def term(e, m, g, zs, place):
+        first = zs * 2 * PAIR + g * PAIR
+        return jnp.dot(att[g, zs, place, :], outw[e, m, first : first + PAIR, :], preferred_element_type=jnp.float32)
+
+    def premix():
+        for m in range(PLANE):
+            premixed[m] = sum(term(1, m, g, zs, slice(None)) for zs in range(1, last) for g in range(2))
 
     def mix_block(e, b):
         place = pl.ds(pl.multiple_of(b * span, span), span)
         owner = own_end if e == 0 else z
         for h in range(halves):
             for m in range(h * each, (h + 1) * each):
-                total = None
-                for zs in range(depth):
-                    for g in range(2):
-                        first = zs * 2 * PAIR + g * PAIR
-                        term = jnp.dot(
-                            att[g, zs, place, :],
-                            outw[e, m, first : first + PAIR, :],
-                            preferred_element_type=jnp.float32,
-                        )
-                        total = term if total is None else total + term
+                total = sum(term(e, m, g, zs, place) for zs in ((0, last) if e else range(depth)) for g in range(2))
+                if e:
+                    total = total + premixed[m, place, :]
                 value = total.astype(jnp.bfloat16)
 
                 @pl.when(b == z)
@@ -562,20 +573,31 @@
             go.remote(block, block, out_side_sem.at[e], sibling).start()
 
         side_columns(1)
-        for g in range(2):
-            for i in range(depth):
-                hand_on(g, i)
+        for i in range(depth):
+            hand_on(0, i)
         go.arrive(outw.at[1, pl.ds(0, CORES)], out_side_sem.at[1])
         for i in range(depth):
-            for zs in (last - z, last - own_end):
-                for g in range(2):
-                    go.arrive(att_piece(g, zs, nth(i)), att_sem.at[g, zs, nth(i)])
+            for g in range(2):
+                go.arrive(att_piece(g, last - z, nth(i)), att_sem.at[g, last - z, nth(i)])
+        premix()
+
+        def mix_own(i):
+            for g in range(2):
+                go.arrive(att_piece(g, last - own_end, nth(i)), att_sem.at[g, last - own_end, nth(i)])
             mix_block(1, nth(i))
-            if i == 1:
-                side_columns(0)
+
+        for i in range(depth - 1):
+            hand_on(1, i)
+        mix_own(0)
+        hand_on(1, depth - 1)
+        mix_own(1)
+        side_columns(0)
+        mix_own(2)
         go.arrive(outw.at[0, pl.ds(0, CORES)], out_side_sem.at[0])
-        for i in range(depth):
+        for i in range(depth - 1):
             mix_block(0, nth(i))
+        mix_own(depth - 1)
+        mix_block(0, nth(depth - 1))
 
     go.count(outw.at[0, 0], inner, times=2)
     go.count(att.at[:, 0], inner)
@@ -645,9 +667,9 @@
         out_specs=(hbm, vmem, vmem),
         scratch_shapes=[
             bf16(depth, 2, span, half_width),
-            bf16(depth, span, 2 * half_width),
+            bf16(CORES, depth, span, half_width),
             bf16(2, half_width // HEAD_SIZE, HEAD_SIZE),
-            bf16(3, n_seq, slab, PAIR),
+            bf16(3, CORES, n_seq // CORES, slab, PAIR),
             bf16(2, PLANE, w_out.shape[0], width),
             bf16(PLANE, tokens, PAIR),
             bf16(2, depth, 2 * span, HEAD_SIZE),
@@ -663,10 +685,12 @@
             f32(2, 1, half_width),
             f32(half_width // HEAD_SIZE, HEAD_SIZE),
             bf16(2, HEAD_SIZE),
+            f32(tokens, PAIR),
+            f32(PLANE, tokens, width),
             f32(span, half_width),
-            bf16(5120, half_width),
+            bf16(3072, half_width),
             dma((5,)),
-            dma((1,)),
+            dma((2,)),
             dma((4,)),
             dma((1,)),
             dma((depth, PIECES)),
@@ -679,8 +703,8 @@
             dma((2,)),
             dma((2,)),
             dma((2, depth, depth)),
-            dma((depth, 2)),
-            dma((depth // 2, 2)),
+            dma((depth, PLANE)),
+            dma((depth // 2, PLANE)),
         ],
         compiler_params=pltpu.CompilerParams(
             collective_id=0, has_side_effects=True, vmem_limit_bytes=60 * 1024 * 1024

time: 134 us -> 130 us (0.970)
  Pallas kernels: 129 us -> 126 us
    pallas_call x1, Pallas kernels: 129 us -> 126 us  [per_device_by_column(): pl.pallas_call(lambda *refs: column_kernel(depth, *refs), out_shape=(f32_...]
where the time goes in v5:
time: 130 us
  Pallas kernels  126 us (97%)
  other arithmetic  2.78 us (2%)
    pallas_call x1, Pallas kernels, per_device_by_column(): pl.pallas_call(lambda *refs: column_kernel(depth, *refs), out_shape=(f32_...  126 us
    convert_element_type x1, other arithmetic, per_device_by_column(): normed = (stream * factor.reshape(span, 1) * post).astype(jnp.bfloat16)  2.78 us

profile of v5, /device:TPU:8, one launch (start us, length us, event | category | flops | bytes accessed | tf_op | source)
XLA Modules:
  0.0 130.3 jit_solution(7288546442491595908)
XLA Ops:
  0.6 0.0 copy-start
  0.6 126.1 %sublayer.1 = (f32[128,2048]{1,0:T(8,128)}, f32[1,128]{1,0:T(1,128)}, f32[1,2048]{1,0:T(1,128)}) custom-call(bf16[128,2048]{1,0:T(8,128)(2,1)} %refs_0_.1, s32[16]{0:T(128)} %refs_1_.1, bf16[16,128]{1,0:T(8,128)(2,1)} %bitcast.6, bf16[16,128]{1,0:T(8,128)(2,1)} %bitcast.7, bf16[16,128]{1,0:T(8,128)(2,1)} %bitcast.8, bf16[256,2048]{1,0:T(8,128)(2,1)} %refs_5_.1, ...), custom_call_target="tpu_custom_call" | custom-call | tf_op jit(solution)/shard_map/sublayer/pallas_call | solution.py:663
  126.8 0.0 copy-start.1
  126.8 0.0 copy-start.2
  126.8 0.0 copy-done
  126.8 0.7 copy-done.1
  127.5 0.0 copy-done.2
  127.5 2.8 %multiply_convert_fusion = (bf16[128,2048]{1,0:T(8,128)(2,1)}, bf16[128,2048]{1,0:T(8,128)(2,1)}) fusion(f32[128,2048]{1,0:T(8,128)} %get-tuple-element.5, bf16[128,2048]{1,0:T(8,128)(2,1)S(1)} %copy-done, f32[2048]{0:T(1024)S(1)} %bitcast.5, f32[128]{0:T(128)S(1)} %bitcast.9), kind=kLoop, calls=%fused_computation | loop fusion | flops 1572864 | bytes 2630144 | tf_op jit(solution)/shard_map/convert_element_type | solution.py:725
Async XLA Ops:
  0.6 126.2 %copy-start = (bf16[128,2048]{1,0:T(8,128)(2,1)S(1)}, bf16[128,2048]{1,0:T(8,128)(2,1)}, u32[]{:S(2)}) copy-start(bf16[128,2048]{1,0:T(8,128)(2,1)} %refs_0_.1) | copy-start | bytes 1572868
  126.8 0.7 copy-start.1
  126.8 0.7 copy-start.2

commit v6 on v5

--- a/solution.py
+++ b/solution.py
@@ -233,7 +233,7 @@
     rows, full, gains, weights, outw, kvs, queries, att, part, terms, others, squares,
     kv_pieces, cos_t, sin_t, key_pos, gain_rows, bias_b, bias_p, early, premixed, mixed_rows, proxy,
     local_sem, send_sem, small_sem, relay_sem, rows_sem, rows_side_sem,
-    w_sem, w_across_sem, w_side_sem, out_end_sem, out_across_sem, out_side_sem, kv_sem, att_sem, term_sem, other_sem,
+    w_sem, w_across_sem, w_side_sem, out_end_sem, out_across_sem, out_side_sem, kv_sem, att_sem, term_sem, other_sem, cross_sem,
 ):
     s, t = lax.axis_index("seq"), lax.axis_index("tp")
     z, x, c = s // PLANE, s % PLANE // CORES, s % CORES
@@ -246,6 +246,7 @@
 
     barrier = pltpu.get_barrier_semaphore()
     peers = [sibling, across, other] + [(at(lax.rem(z + d, depth), x, c), t) for d in range(1, depth)]
+    peers += [(at(lax.rem(z + d, depth), x, c), 1 - t) for d in range(1, depth)]
     for peer in peers:
         pl.semaphore_signal(barrier, inc=1, device_id=peer, device_id_type=MESH)
     pl.semaphore_wait(barrier, len(peers))
@@ -298,11 +299,18 @@
         landing = outw.at[0, column, place]
         go.send(w_out.at[place], landing, out_end_sem.at[0], (at(gatherer, x, c), t), outer)
 
-    def spread(stage, groups):
+    def spread(stage, groups, least=1):
         for g in groups:
-            for zt, where in ((stage, lambda k: k < stage), (last - stage, lambda k: k > last - stage)):
+            for zt, where in (
+                (stage, lambda k: k <= stage - least),
+                (last - stage, lambda k: k >= last - stage + least),
+            ):
                 source = kv_pieces.at[zt] if g == 0 else q_piece(g, zt)
                 go.send(source, weights.at[g, c, s // CORES], w_sem.at[g, z], (at(zt, x, c), t), where)
+
+    def spread_near(stage, g):
+        for zt, source in ((stage, stage - 1), (last - stage, last - stage + 1)):
+            go.send(q_piece(g, zt), weights.at[g, c, s // CORES], w_sem.at[g, z], (at(zt, x, c), t), lambda k: k == source)
 
     def take_weights(g, stage, distances=None):
         for distance in distances or range(1, stage + 1):
@@ -405,6 +413,7 @@
     pass_rows(1)
     spread(1, (0, 1, 2))
     spread(3, (0,))
+    spread_near(3, 1)
     leave_columns(0)
     normalize(z)
     pass_rows(2)
@@ -413,14 +422,15 @@
         take_weights(g, 1)
     normalize(z + 1 - 2 * lax.rem(z, 2))
     take_weights(0, 3)
+    take_weights(1, 3, (1,))
     take_weights(0, 2)
     go.left(rows.at[z, t], relay_sem.at[0], middle)
     pass_rows(3)
-    spread(3, (1,))
+    spread(3, (1,), 2)
     leave_columns(1)
     take_weights(1, 2)
     normalize(lax.rem(z + 2, depth))
-    take_weights(1, 3, (1, 2))
+    take_weights(1, 3, (2, 3))
     normalize(last - z)
     weights_across(0)
 
@@ -450,7 +460,6 @@
     go.send(kv_block(column), kv_block(column), kv_sem.at[1], sibling)
     spread(3, (2,))
     take_weights(2, 2)
-    take_weights(1, 3, (3,))
     take_weights(2, 3)
 
     go.epoch = 1
@@ -560,10 +569,23 @@
                 def _():
                     part[e, b, m] = value
 
-            @pl.when(b != z)
+            index = lax.rem(owner, share)
+            stays = owner // share == t
+
+            @pl.when(jnp.logical_and(b != z, stays))
             def _():
                 source = piece(part.at[e], b, h)
                 go.remote(source, piece(terms, owner, h), term_sem.at[owner, h], (at(b, x, c), t)).start()
+
+            @pl.when(jnp.logical_and(b != z, jnp.logical_not(stays)))
+            def _():
+                source = piece(part.at[e], b, h)
+                go.remote(source, piece(others, index, h), other_sem.at[index, h], (at(b, x, c), 1 - t)).start()
+
+            @pl.when(jnp.logical_and(b == z, jnp.logical_not(stays)))
+            def _():
+                source = piece(terms, owner, h)
+                go.remote(source, piece(others, index, h), other_sem.at[index, h], other, cross_sem.at[0]).start()
 
     @pl.when(middle)
     def _():
@@ -603,23 +625,16 @@
     go.count(att.at[:, 0], inner)
     go.count(part.at[0, 0], inner, times=2 * (depth - 1))
 
-    near = jnp.where(z < share, 0, share)
-    for e in (1, 0):
-        for h in range(halves):
-            for first in (near, share - near):
-                maker = jnp.where(first == 0, 1, last - 1)
-                index = jnp.where(first == 0, e, 1 - e)
-                block = piece(terms, first + index, h)
-                go.arrive(block, term_sem.at[first + index, h], z != maker)
-                go.send(block, piece(others, index, h), other_sem.at[index, h], other, also=t != first // share)
-    go.count(others.at[0], times=share)
-
+    crosses = jnp.logical_and(middle, t != z // share)
+    maker = jnp.where(t == 0, 1, last - 1)
     width = w_out.shape[1]
     sums = jnp.zeros((span, 1), jnp.float32)
     pieces = [(j, m) for j in range(share) for m in range(PLANE)]
     for j, m in pieces:
         if m % each == 0:
-            go.arrive(piece(others, j, m // each), other_sem.at[j, m // each])
+            h = m // each
+            go.arrive(piece(terms, t * share + j, h), term_sem.at[t * share + j, h], z != maker)
+            go.arrive(piece(others, j, h), other_sem.at[j, h])
         cut = slice((j * PLANE + m) * width, (j * PLANE + m + 1) * width)
         mixed = terms[t * share + j, m].astype(jnp.float32) + others[j, m].astype(jnp.float32)
         mixed_rows[:, cut] = mixed
@@ -633,6 +648,7 @@
     total = (squares[0] + squares[1])[:1]
     factor_out[...] = lax.rsqrt(total / (2 * half_width) + eps)
     write.wait()
+    go.left(others, cross_sem.at[0], crosses)
     go.left(gain, small_sem.at[1])
     go.left(squares.at[t], small_sem.at[3])
     go.finish()
@@ -705,6 +721,7 @@
             dma((2, depth, depth)),
             dma((depth, PLANE)),
             dma((depth // 2, PLANE)),
+            dma((1,)),
         ],
         compiler_params=pltpu.CompilerParams(
             collective_id=0, has_side_effects=True, vmem_limit_bytes=60 * 1024 * 1024

time: 130 us -> 127 us (0.977)
  Pallas kernels: 126 us -> 123 us
    pallas_call x1, Pallas kernels: 126 us -> 123 us  [per_device_by_column(): pl.pallas_call(lambda *refs: column_kernel(depth, *refs), out_shape=(f32_...]
where the time goes in v6:
time: 127 us
  Pallas kernels  123 us (97%)
  other arithmetic  2.78 us (2%)
    pallas_call x1, Pallas kernels, per_device_by_column(): pl.pallas_call(lambda *refs: column_kernel(depth, *refs), out_shape=(f32_...  123 us
    convert_element_type x1, other arithmetic, per_device_by_column(): normed = (stream * factor.reshape(span, 1) * post).astype(jnp.bfloat16)  2.78 us

profile of v6, /device:TPU:8, one launch (start us, length us, event | category | flops | bytes accessed | tf_op | source)
XLA Modules:
  0.0 127.1 jit_solution(17944713494672588722)
XLA Ops:
  0.6 0.0 copy-start
  0.6 123.0 %sublayer.1 = (f32[128,2048]{1,0:T(8,128)}, f32[1,128]{1,0:T(1,128)}, f32[1,2048]{1,0:T(1,128)}) custom-call(bf16[128,2048]{1,0:T(8,128)(2,1)} %refs_0_.1, s32[16]{0:T(128)} %refs_1_.1, bf16[16,128]{1,0:T(8,128)(2,1)} %bitcast.6, bf16[16,128]{1,0:T(8,128)(2,1)} %bitcast.7, bf16[16,128]{1,0:T(8,128)(2,1)} %bitcast.8, bf16[256,2048]{1,0:T(8,128)(2,1)} %refs_5_.1, ...), custom_call_target="tpu_custom_call" | custom-call | tf_op jit(solution)/shard_map/sublayer/pallas_call | solution.py:679
  123.6 0.0 copy-start.1
  123.6 0.0 copy-start.2
  123.7 0.0 copy-done
  123.7 0.7 copy-done.1
  124.3 0.0 copy-done.2
  124.3 2.8 %multiply_convert_fusion = (bf16[128,2048]{1,0:T(8,128)(2,1)}, bf16[128,2048]{1,0:T(8,128)(2,1)}) fusion(f32[128,2048]{1,0:T(8,128)} %get-tuple-element.5, bf16[128,2048]{1,0:T(8,128)(2,1)S(1)} %copy-done, f32[2048]{0:T(1024)S(1)} %bitcast.5, f32[128]{0:T(128)S(1)} %bitcast.9), kind=kLoop, calls=%fused_computation | loop fusion | flops 1572864 | bytes 2630144 | tf_op jit(solution)/shard_map/convert_element_type | solution.py:742
Async XLA Ops:
  0.6 123.0 %copy-start = (bf16[128,2048]{1,0:T(8,128)(2,1)S(1)}, bf16[128,2048]{1,0:T(8,128)(2,1)}, u32[]{:S(2)}) copy-start(bf16[128,2048]{1,0:T(8,128)(2,1)} %refs_0_.1) | copy-start | bytes 1572868
  123.6 0.7 copy-start.1
  123.6 0.7 copy-start.2

commit v7 on v6

--- a/solution.py
+++ b/solution.py
@@ -164,7 +164,7 @@
 MESH = pl.DeviceIdType.MESH
 CORES = 2
 PLANE = 4
-PIECES = 2
+PIECES = 4
 PAIR = 2 * HEAD_SIZE
 
 

time: 127 us -> 127 us (level)
  no operation moved by 1% of the time
where the time goes in v7:
time: 127 us
  Pallas kernels  123 us (97%)
  other arithmetic  2.78 us (2%)
    pallas_call x1, Pallas kernels, per_device_by_column(): pl.pallas_call(lambda *refs: column_kernel(depth, *refs), out_shape=(f32_...  123 us
    convert_element_type x1, other arithmetic, per_device_by_column(): normed = (stream * factor.reshape(span, 1) * post).astype(jnp.bfloat16)  2.78 us

profile of v7, /device:TPU:8, one launch (start us, length us, event | category | flops | bytes accessed | tf_op | source)
XLA Modules:
  0.0 127.2 jit_solution(9157221652310184407)
XLA Ops:
  0.6 0.0 copy-start
  0.6 123.1 %sublayer.1 = (f32[128,2048]{1,0:T(8,128)}, f32[1,128]{1,0:T(1,128)}, f32[1,2048]{1,0:T(1,128)}) custom-call(bf16[128,2048]{1,0:T(8,128)(2,1)} %refs_0_.1, s32[16]{0:T(128)} %refs_1_.1, bf16[16,128]{1,0:T(8,128)(2,1)} %bitcast.6, bf16[16,128]{1,0:T(8,128)(2,1)} %bitcast.7, bf16[16,128]{1,0:T(8,128)(2,1)} %bitcast.8, bf16[256,2048]{1,0:T(8,128)(2,1)} %refs_5_.1, ...), custom_call_target="tpu_custom_call" | custom-call | tf_op jit(solution)/shard_map/sublayer/pallas_call | solution.py:679
  123.7 0.0 copy-start.1
  123.7 0.0 copy-start.2
  123.7 0.0 copy-done
  123.7 0.7 copy-done.1
  124.4 0.0 copy-done.2
  124.4 2.8 %multiply_convert_fusion = (bf16[128,2048]{1,0:T(8,128)(2,1)}, bf16[128,2048]{1,0:T(8,128)(2,1)}) fusion(f32[128,2048]{1,0:T(8,128)} %get-tuple-element.5, bf16[128,2048]{1,0:T(8,128)(2,1)S(1)} %copy-done, f32[2048]{0:T(1024)S(1)} %bitcast.5, f32[128]{0:T(128)S(1)} %bitcast.9), kind=kLoop, calls=%fused_computation | loop fusion | flops 1572864 | bytes 2630144 | tf_op jit(solution)/shard_map/convert_element_type | solution.py:742
Async XLA Ops:
  0.6 123.1 %copy-start = (bf16[128,2048]{1,0:T(8,128)(2,1)S(1)}, bf16[128,2048]{1,0:T(8,128)(2,1)}, u32[]{:S(2)}) copy-start(bf16[128,2048]{1,0:T(8,128)(2,1)} %refs_0_.1) | copy-start | bytes 1572868
  123.7 0.7 copy-start.1
  123.7 0.7 copy-start.2
